TPU v7x, 1024 devices: a whole 4x4x32 slice. The times are simulated.
1024 devices in a mesh: gx: 32 (over z), gy: 32 (over x, y, core).
Axes of the slice: x: 4, y: 4, z: 32, core: 2. Of those that a mesh axis runs over, the one named last changes fastest.
Arguments:
- conductivity: float32 [1024, 1024, 128], P('gx', 'gy'), may hold values from 0.25 to 4
- source: float32 [1024, 1024, 128], P('gx', 'gy'), may hold values from -12 to 12
- initial: float32 [1024, 1024, 128], P('gx', 'gy'), may hold values from -3 to 3
Outputs:
- solution: float32 [1024, 1024, 128], P('gx', 'gy')
All inputs are finite; a program needn't handle non-finite values.
Results may differ from a plain program's by a relative error of at most 0.0003.
Values sent between devices are 32-bit elements; how exact they have to be, the bound alone decides.
No kernel may reach another device: no remote copies, remote signals or barrier semaphores. Data moves between devices by JAX's collectives and lax.ppermute only.
A program may use at most 32 MiB of HBM per device.

v0:
```python
import jax
import jax.numpy as jnp
from jax import lax
from jax.sharding import PartitionSpec as P

NU = 3
CG_ITERS = 32


relax_weight = 0.8


def extended(cells, sides, width):
    for axis, dim in sides:
        count = lax.axis_size(axis)
        ends = count - 1
        head = lax.slice_in_dim(cells, 0, width, axis=dim)
        tail = lax.slice_in_dim(cells, cells.shape[dim] - width, cells.shape[dim], axis=dim)
        cells = jnp.concatenate(
            [
                lax.ppermute(tail, axis, [(i, (i + 1) % count) for i in range(ends)]),
                cells,
                lax.ppermute(head, axis, [((i + 1) % count, i) for i in range(ends)]),
            ],
            axis=dim,
        )
    return cells


def turned_gather(arrays, axis, dims):
    turned = [jnp.moveaxis(a, dim, 0) for a, dim in zip(arrays, dims)]
    widths = [t[0].size for t in turned]
    both = jnp.concatenate([t.reshape(-1, w) for t, w in zip(turned, widths)], axis=1)
    filled = lax.all_gather(both, axis, axis=0, tiled=True)
    blocks = jnp.split(filled, [sum(widths[:k]) for k in range(1, len(widths))], axis=1)
    return tuple(
        (
            jnp.moveaxis(b.reshape(-1, *t.shape[1:]), 0, dim)
            for b, t, dim in zip(blocks, turned, dims)
        )
    )


def laid_out(blocks, dim):
    lengths = list(blocks.shape[1:])
    lengths[dim] *= blocks.shape[0]
    return jnp.moveaxis(blocks, 0, dim).reshape(lengths)


def gather_together(arrays, axis, dims):
    vector = jnp.concatenate([a.reshape(-1) for a in arrays])
    lines, at, outs = (lax.all_gather(vector, axis), 0, [])
    for a, dim in zip(arrays, dims):
        blocks = lines[:, at : at + a.size].reshape(-1, *a.shape)
        outs.append(laid_out(blocks, dim))
        at += a.size
    return tuple(outs)


def operate(padded, cond_pad):
    center_cond = cond_pad[1:-1, 1:-1]
    center = padded[1:-1, 1:-1]
    face_east = 0.5 * (center_cond + cond_pad[2:, 1:-1])
    face_west = 0.5 * (center_cond + cond_pad[:-2, 1:-1])
    face_north = 0.5 * (center_cond + cond_pad[1:-1, 2:])
    face_south = 0.5 * (center_cond + cond_pad[1:-1, :-2])
    between = 0.5 * (center_cond[:, :, 1:] + center_cond[:, :, :-1])
    zero_plane = jnp.zeros(center.shape[:2] + (1,), center.dtype)
    face_up = jnp.concatenate([between, zero_plane], 2)
    face_down = jnp.concatenate([zero_plane, between], 2)
    value_up = jnp.concatenate([center[:, :, 1:], zero_plane], 2)
    value_down = jnp.concatenate([zero_plane, center[:, :, :-1]], 2)
    diagonal = face_east + face_west + face_north + face_south + face_up + face_down
    neighbor_sum = (
        face_east * padded[2:, 1:-1]
        + face_west * padded[:-2, 1:-1]
        + face_north * padded[1:-1, 2:]
        + face_south * padded[1:-1, :-2]
        + face_up * value_up
        + face_down * value_down
    )
    return (diagonal * center - neighbor_sum, diagonal, center_cond, center)


def smooth_once(padded, cond_pad, source):
    applied, diagonal, center_cond, center = operate(padded, cond_pad)
    inside = center_cond > 0
    update = relax_weight * (source - applied) / jnp.where(inside, diagonal, 1.0)
    return jnp.where(inside, center + update, 0.0)


def coarse_apply(estimate, coarse_diag, flow_east, flow_north):
    edge_rows = jnp.zeros((1, estimate.shape[1]), estimate.dtype)
    edge_cols = jnp.zeros((estimate.shape[0], 1), estimate.dtype)
    ahead_x = jnp.concatenate([estimate[1:], edge_rows], 0)
    carried_x = flow_east * estimate
    behind_x = jnp.concatenate([edge_rows, carried_x[:-1]], 0)
    ahead_y = jnp.concatenate([estimate[:, 1:], edge_cols], 1)
    carried_y = flow_north * estimate
    behind_y = jnp.concatenate([edge_cols, carried_y[:, :-1]], 1)
    return coarse_diag * estimate - flow_east * ahead_x - behind_x - flow_north * ahead_y - behind_y


def coarse_solve(coarse_source, coarse_diag, flow_east, flow_north):

    def iterate_once(counter, carried):
        estimate, remainder, search, norm_now = carried
        product = coarse_apply(search, coarse_diag, flow_east, flow_north)
        alpha_step = norm_now / jnp.sum(search * product)
        estimate = estimate + alpha_step * search
        remainder = remainder - alpha_step * product
        norm_next = jnp.sum(remainder * remainder)
        search = remainder + norm_next / norm_now * search
        return (estimate, remainder, search, norm_next)

    start_state = (
        jnp.zeros_like(coarse_source),
        coarse_source,
        coarse_source,
        jnp.sum(coarse_source * coarse_source),
    )
    return lax.fori_loop(0, CG_ITERS, iterate_once, start_state)[0]


def trim_rim(array, width, depth):
    cut = depth - width
    return array[cut : array.shape[0] - cut, cut : array.shape[1] - cut]


def relax_deep(padded, width, cond_big, source_big, sweeps, depth):
    for repeat in range(sweeps):
        current = width - repeat
        padded = smooth_once(
            padded, trim_rim(cond_big, current, depth), trim_rim(source_big, current - 1, depth)
        )
    return padded


def body(conductivity, source, initial):
    extent_x = conductivity.shape[0]
    extent_y = conductivity.shape[1]
    depth = NU + 1
    stacked = extended(jnp.stack([conductivity, source, initial]), (("gx", 1), ("gy", 2)), depth)
    padded = relax_deep(stacked[2], depth, stacked[0], stacked[1], NU, depth)
    cond_pad = trim_rim(stacked[0], 1, depth)
    applied = operate(padded, cond_pad)[0]
    iterate = padded[1:-1, 1:-1]
    remainder = source - applied
    coarse_source = jnp.sum(remainder).reshape(1)
    flow_east = jnp.sum(0.5 * (cond_pad[extent_x, 1:-1] + cond_pad[extent_x + 1, 1:-1])).reshape(1)
    flow_west = jnp.sum(0.5 * (cond_pad[1, 1:-1] + cond_pad[0, 1:-1])).reshape(1)
    flow_north = jnp.sum(0.5 * (cond_pad[1:-1, extent_y] + cond_pad[1:-1, extent_y + 1])).reshape(1)
    flow_south = jnp.sum(0.5 * (cond_pad[1:-1, 1] + cond_pad[1:-1, 0])).reshape(1)
    coarse_diag = flow_east + flow_west + flow_north + flow_south
    along_rows = turned_gather(
        (coarse_source, coarse_diag, flow_east, flow_north), "gy", (0, 0, 0, 0)
    )
    gathered = gather_together(
        (along_rows[0], along_rows[1], along_rows[2], along_rows[3]), "gx", (0, 0, 0, 0)
    )
    count_x = lax.axis_size("gx")
    count_y = lax.axis_size("gy")
    correction = coarse_solve(
        gathered[0].reshape(count_x, count_y),
        gathered[1].reshape(count_x, count_y),
        gathered[2].reshape(count_x, count_y),
        gathered[3].reshape(count_x, count_y),
    )
    index_x = lax.axis_index("gx")
    index_y = lax.axis_index("gy")
    own_share = lax.dynamic_slice(correction, (index_x, index_y), (1, 1))[0, 0]
    iterate = iterate + own_share
    refreshed = extended(iterate, (("gx", 0), ("gy", 1)), NU)
    iterate = relax_deep(refreshed, NU, stacked[0], stacked[1], NU, depth)
    return iterate


def solution(mesh):
    return jax.shard_map(
        body,
        mesh=mesh,
        in_specs=(P("gx", "gy", None), P("gx", "gy", None), P("gx", "gy", None)),
        out_specs=P("gx", "gy", None),
        check_vma=False,
    )
```

profile of v0, /device:TPU:36, one launch (start us, length us, event | category | flops | bytes accessed | tf_op | source)
XLA Modules:
  0.0 308.0 jit_solution(14683771332667776640)
XLA Ops:
  1.2 2.0 collective-permute-start.1
  3.2 3.8 %collective-permute-start = (f32[3,4,32,128]{3,2,1,0:T(8,128)S(1)}, f32[3,4,32,128]{3,2,1,0:T(8,128)S(1)}, u32[]{:S(2)}, u32[]{:S(2)}) collective-permute-start(f32[3,4,32,128]{3,2,1,0:T(8,128)S(1)} %get-tuple-element.114), channel_id=1, source_target_pairs={{0,32},{32,64},{64,96},{96,128},{128,160},{160,192},{192,224},{224... | collective-permute-start | bytes 589832 | tf_op jit(solution)/shard_map/ppermute | solution.py:21
  7.0 2.9 collective-permute-done.1
  9.9 1.7 collective-permute-done
  12.9 3.4 %collective-permute-start.3 = (f32[3,40,4,128]{3,2,1,0:T(4,128)S(1)}, f32[3,40,4,128]{3,2,1,0:T(4,128)S(1)}, u32[]{:S(2)}, u32[]{:S(2)}) collective-permute-start(f32[3,40,4,128]{3,2,1,0:T(4,128)S(1)} %get-tuple-element.113), channel_id=1, source_target_pairs={{1,0},{2,1},{3,2},{4,3},{5,4},{6,5},{7,6},{8,7},{9,8},{10,9},{11,1... | collective-permute-start | bytes 737288 | tf_op jit(solution)/shard_map/ppermute | solution.py:23
  16.3 1.9 collective-permute-start.2
  18.3 1.8 collective-permute-done.3
  20.0 5.9 %collective-permute-done.2 = f32[3,40,4,128]{3,2,1,0:T(4,128)S(1)} collective-permute-done((f32[3,40,4,128]{3,2,1,0:T(4,128)S(1)}, f32[3,40,4,128]{3,2,1,0:T(4,128)S(1)}, u32[]{:S(2)}, u32[]{:S(2)}) %collective-permute-start.2) | collective-permute-done | bytes 245792 | tf_op jit(solution)/shard_map/ppermute | solution.py:21
  30.0 1.4 fusion.8
  31.6 2.0 fusion.35
  33.8 1.9 fusion.63
  39.5 3.0 fusion.88
  42.4 2.0 maximum_bitcast_fusion
  44.4 27.0 %all-gather.1 = f32[32,1,4]{2,1,0:T(1,128)S(1)} all-gather(f32[1,1,4]{2,1,0:T(1,128)S(1)} %maximum_bitcast_fusion), channel_id=1, replica_groups=mesh['gx'=32,'gy'=32] {'gy'}, dimensions={0}, use_global_device_ids=true | all-gather | bytes 528 | tf_op jit(solution)/shard_map/all_gather | solution.py:34
  71.6 61.2 %all-gather.2 = f32[32,1,128]{2,1,0:T(1,128)S(1)} all-gather(f32[1,1,128]{2,1,0:T(1,128)S(1)} %maximum_bitcast_fusion.1), channel_id=2, replica_groups=mesh['gx'=32,'gy'=32] {'gx'}, dimensions={0}, use_global_device_ids=true | all-gather | bytes 16896 | tf_op jit(solution)/shard_map/all_gather | solution.py:52
  133.4 147.0 %while.17 = (s32[]{:T(128)}, f32[32,32]{1,0:T(8,128)}, f32[32,32]{1,0:T(8,128)S(1)}, f32[32,32]{1,0:T(8,128)S(1)}, f32[]{:T(128)}, /*index=5*/f32[32,32]{1,0:T(8...) while((s32[]{:T(128)}, f32[32,32]{1,0:T(8,128)}, ...), condition=%wide.region_9.10_spmd.clone, body=%wide.region_6.9_spmd.clone.sunk | while | flops 20419 | bytes 108971 | solution.py:122
  282.4 2.9 collective-permute-start.5
  285.4 3.0 collective-permute-start.4
  288.4 3.1 collective-permute-done.4
  291.5 1.9 collective-permute-start.7
  293.4 2.6 collective-permute-start.6
  296.0 5.2 %collective-permute-done.6 = f32[38,3,128]{2,1,0:T(4,128)S(1)} collective-permute-done((f32[38,3,128]{2,1,0:T(4,128)S(1)}, f32[38,3,128]{2,1,0:T(4,128)S(1)}, u32[]{:S(2)}, u32[]{:S(2)}) %collective-permute-start.6) | collective-permute-done | bytes 58400 | tf_op jit(solution)/shard_map/ppermute | solution.py:21
  301.7 1.3 fusion.24
  306.2 1.7 fusion.80
  (206 shorter events, 100.2 us)
Async XLA Ops:
  0.0 25.9 %copy-start.3 = (f32[32,32,128]{2,1,0:T(8,128)S(1)}, f32[32,32,128]{2,1,0:T(8,128)}, u32[]{:S(2)}) copy-start(f32[32,32,128]{2,1,0:T(8,128)} %param.7) | copy-start | bytes 1572868
  0.0 25.9 %copy-start = (f32[32,32,128]{2,1,0:T(8,128)S(1)}, f32[32,32,128]{2,1,0:T(8,128)}, u32[]{:S(2)}) copy-start(f32[32,32,128]{2,1,0:T(8,128)} %param.6) | copy-start | bytes 1572868
  0.0 25.9 %copy-start.4 = (f32[32,32,128]{2,1,0:T(8,128)S(1)}, f32[32,32,128]{2,1,0:T(8,128)}, u32[]{:S(2)}) copy-start(f32[32,32,128]{2,1,0:T(8,128)} %param.5) | copy-start | bytes 1572868
  1.2 8.7 %collective-permute-start.1 = (f32[3,4,32,128]{3,2,1,0:T(8,128)S(1)}, f32[3,4,32,128]{3,2,1,0:T(8,128)S(1)}, u32[]{:S(2)}, u32[]{:S(2)}) collective-permute-start(f32[3,4,32,128]{3,2,1,0:T(8,128)S(1)} %get-tuple-element.115), channel_id=1, source_target_pairs={{32,0},{64,32},{96,64},{128,96},{160,128},{192,160},{224,192},{256... | collective-permute-start | bytes 589832 | tf_op jit(solution)/shard_map/ppermute | solution.py:23
  3.2 8.4 %collective-permute-start = (f32[3,4,32,128]{3,2,1,0:T(8,128)S(1)}, f32[3,4,32,128]{3,2,1,0:T(8,128)S(1)}, u32[]{:S(2)}, u32[]{:S(2)}) collective-permute-start(f32[3,4,32,128]{3,2,1,0:T(8,128)S(1)} %get-tuple-element.114), channel_id=1, source_target_pairs={{0,32},{32,64},{64,96},{96,128},{128,160},{160,192},{192,224},{224... | collective-permute-start | bytes 589832 | tf_op jit(solution)/shard_map/ppermute | solution.py:21
  12.9 7.1 %collective-permute-start.3 = (f32[3,40,4,128]{3,2,1,0:T(4,128)S(1)}, f32[3,40,4,128]{3,2,1,0:T(4,128)S(1)}, u32[]{:S(2)}, u32[]{:S(2)}) collective-permute-start(f32[3,40,4,128]{3,2,1,0:T(4,128)S(1)} %get-tuple-element.113), channel_id=1, source_target_pairs={{1,0},{2,1},{3,2},{4,3},{5,4},{6,5},{7,6},{8,7},{9,8},{10,9},{11,1... | collective-permute-start | bytes 737288 | tf_op jit(solution)/shard_map/ppermute | solution.py:23
  16.3 9.6 %collective-permute-start.2 = (f32[3,40,4,128]{3,2,1,0:T(4,128)S(1)}, f32[3,40,4,128]{3,2,1,0:T(4,128)S(1)}, u32[]{:S(2)}, u32[]{:S(2)}) collective-permute-start(f32[3,40,4,128]{3,2,1,0:T(4,128)S(1)} %get-tuple-element.112), channel_id=1, source_target_pairs={{0,1},{1,2},{2,3},{3,4},{4,5},{5,6},{6,7},{7,8},{8,9},{9,10},{10,1... | collective-permute-start | bytes 737288 | tf_op jit(solution)/shard_map/ppermute | solution.py:21
  26.8 4.8 %copy-start.1 = (f32[36,36,127]{2,1,0:T(8,128)}, f32[36,36,127]{2,1,0:T(8,128)S(1)}, u32[]{:S(2)}) copy-start(f32[36,36,127]{2,1,0:T(8,128)S(1)} %fusion.38) | copy-start | bytes 1975108
  282.4 6.0 %collective-permute-start.5 = (f32[3,32,128]{2,1,0:T(8,128)S(1)}, f32[3,32,128]{2,1,0:T(8,128)S(1)}, u32[]{:S(2)}, u32[]{:S(2)}) collective-permute-start(f32[3,32,128]{2,1,0:T(8,128)S(1)} %get-tuple-element.133), channel_id=1, source_target_pairs={{32,0},{64,32},{96,64},{128,96},{160,128},{192,160},{224,192},{256... | collective-permute-start | bytes 147464 | tf_op jit(solution)/shard_map/ppermute | solution.py:23
  285.3 16.3 %copy-start.2 = (f32[36,36,127]{2,1,0:T(8,128)S(1)}, f32[36,36,127]{2,1,0:T(8,128)}, u32[]{:S(2)}) copy-start(f32[36,36,127]{2,1,0:T(8,128)} %copy-done.1) | copy-start | bytes 1975108
  285.4 16.3 %copy-start.6 = (pred[36,36,128]{2,1,0:T(8,128)(4,1)S(1)}, pred[36,36,128]{2,1,0:T(8,128)(4,1)}, u32[]{:S(2)}) copy-start(pred[36,36,128]{2,1,0:T(8,128)(4,1)} %get-tuple-element.102) | copy-start | bytes 497668
  285.4 6.1 %collective-permute-start.4 = (f32[3,32,128]{2,1,0:T(8,128)S(1)}, f32[3,32,128]{2,1,0:T(8,128)S(1)}, u32[]{:S(2)}, u32[]{:S(2)}) collective-permute-start(f32[3,32,128]{2,1,0:T(8,128)S(1)} %get-tuple-element.132), channel_id=1, source_target_pairs={{0,32},{32,64},{64,96},{96,128},{128,160},{160,192},{192,224},{224... | collective-permute-start | bytes 147464 | tf_op jit(solution)/shard_map/ppermute | solution.py:21
  291.5 4.5 %collective-permute-start.7 = (f32[38,3,128]{2,1,0:T(4,128)S(1)}, f32[38,3,128]{2,1,0:T(4,128)S(1)}, u32[]{:S(2)}, u32[]{:S(2)}) collective-permute-start(f32[38,3,128]{2,1,0:T(4,128)S(1)} %get-tuple-element.131), channel_id=1, source_target_pairs={{1,0},{2,1},{3,2},{4,3},{5,4},{6,5},{7,6},{8,7},{9,8},{10,9},{11,1... | collective-permute-start | bytes 175112 | tf_op jit(solution)/shard_map/ppermute | solution.py:23
  293.4 7.8 %collective-permute-start.6 = (f32[38,3,128]{2,1,0:T(4,128)S(1)}, f32[38,3,128]{2,1,0:T(4,128)S(1)}, u32[]{:S(2)}, u32[]{:S(2)}) collective-permute-start(f32[38,3,128]{2,1,0:T(4,128)S(1)} %get-tuple-element.130), channel_id=1, source_target_pairs={{0,1},{1,2},{2,3},{3,4},{4,5},{5,6},{6,7},{7,8},{8,9},{9,10},{10,1... | collective-permute-start | bytes 175112 | tf_op jit(solution)/shard_map/ppermute | solution.py:21
  303.0 0.9 copy-start.7
  305.2 1.0 copy-start.5
where the time goes:
time: 312 us; the launch traced here: 308 us
  other arithmetic  108 us (35%)
  blocking collectives  88.2 us (28%)
  loops' own time  61.3 us (20%)
  starting transfers between devices  21.6 us (7%)
  waiting for transfers between devices  20.6 us (7%)
  local copies, waits for them, and re-layouts  5.41 us (2%)
    another operation x1, loops' own time, coarse_solve(): return lax.fori_loop(0, CG_ITERS, iterate_once, start_state)[0]  61.3 us
    all_gather x1, blocking collectives, gather_together(): lines, at, outs = (lax.all_gather(vector, axis), 0, [])  61.2 us
    add x32, other arithmetic, iterate_once(): search = remainder + norm_next / norm_now * search  41.7 us
    all_gather x1, blocking collectives, turned_gather(): filled = lax.all_gather(both, axis, axis=0, tiled=True)  27 us
    reduce_sum x32, other arithmetic, iterate_once(): alpha_step = norm_now / jnp.sum(search * product)  21.8 us
    reduce_sum x32, other arithmetic, iterate_once(): norm_next = jnp.sum(remainder * remainder)  19.7 us
    ppermute x4, waiting for transfers between devices, extended(): lax.ppermute(tail, axis, [(i, (i + 1) % count) for i in range(ends)])  16 us
    ppermute x4, starting transfers between devices, extended(): lax.ppermute(tail, axis, [(i, (i + 1) % count) for i in range(ends)])  11.4 us
  transfers between devices with their start and end apart: 8, of which 6 were waited for; matrix products, arithmetic and copies ran while one was open for 0% of the time, Pallas kernels for 0%

commit v1 on v0

v1 whole, which is shorter than its diff:
```python
import functools
import jax
import jax.numpy as jnp
from jax import lax
from jax.experimental import pallas as pl
from jax.experimental.pallas import tpu as pltpu
from jax.sharding import PartitionSpec as P

NU = 3
CG_ITERS = 32


relax_weight = 0.8
REACH = 2 * NU
WIDTHS = (REACH, REACH - 1, REACH)
LANES = 128
TILE = 8


def ring_pairs(count, step):
    return [(i, i + step) for i in range(count) if 0 <= i + step < count]


def strip_rows(extent_x):
    rows = []
    for array, width in enumerate(WIDTHS):
        for plane in range(REACH - width, REACH + extent_x + width):
            beyond = max(REACH - plane, plane - (REACH + extent_x - 1), 0)
            if width - beyond > 0:
                rows.append((array, plane, width - beyond))
    return rows


def slab_plane(array, plane, extent_x):
    start = sum(WIDTHS[:array])
    if plane < REACH:
        return 0, start + plane - (REACH - WIDTHS[array])
    return 1, start + plane - (REACH + extent_x)


def strips_kernel(extent_x, low_refs, high_refs, slab_low_refs, slab_high_refs, up_ref, down_ref):
    at = 0
    for array, plane, rows in strip_rows(extent_x):
        if REACH <= plane < REACH + extent_x:
            low, high, where = low_refs[array], high_refs[array], plane - REACH
        else:
            side, where = slab_plane(array, plane, extent_x)
            low, high = slab_low_refs[side], slab_high_refs[side]
        up_ref[at : at + rows, :] = high[where, TILE - rows : TILE, :]
        down_ref[at : at + rows, :] = low[where, 0:rows, :]
        at += rows


def pack_strips(arrays, slabs):
    extent_x, extent_y = arrays[0].shape[:2]
    length = sum(rows for _, _, rows in strip_rows(extent_x))
    last = extent_y // TILE - 1

    def kernel(*refs):
        strips_kernel(extent_x, refs[0:3], refs[3:6], refs[6:8], refs[8:10], *refs[10:])

    def edge(array, block):
        return pl.BlockSpec((array.shape[0], TILE, LANES), lambda i: (0, block, 0))

    return pl.pallas_call(
        kernel,
        grid=(1,),
        in_specs=[edge(a, 0) for a in arrays]
        + [edge(a, last) for a in arrays]
        + [edge(a, 0) for a in slabs]
        + [edge(a, last) for a in slabs],
        out_specs=[pl.BlockSpec((length, LANES), lambda i: (0, 0))] * 2,
        out_shape=[jax.ShapeDtypeStruct((length, LANES), jnp.float32)] * 2,
        name="pack_strips",
    )(*arrays, *arrays, *slabs, *slabs)


def plane_rolls(values, axis):
    return pltpu.roll(values, values.shape[axis] - 1, axis), pltpu.roll(values, 1, axis)


def coefficients(cond, cond_next, face_west, lane):
    face_east = 0.5 * (cond + cond_next)
    face_north = 0.5 * (cond + plane_rolls(cond, 0)[0])
    face_south = plane_rolls(face_north, 0)[1]
    face_up = jnp.where(lane < LANES - 1, 0.5 * (cond + plane_rolls(cond, 1)[0]), 0.0)
    face_down = plane_rolls(face_up, 1)[1]
    diagonal = face_east + face_west + face_north + face_south + face_up + face_down
    scale = jnp.where(cond > 0, relax_weight / diagonal, 0.0)
    return face_east, face_north, face_south, face_up, face_down, scale


def smooth_plane(value, value_next, value_before, faces, source):
    face_east, face_west, face_north, face_south, face_up, face_down, scale = faces
    north, south = plane_rolls(value, 0)
    up, down = plane_rolls(value, 1)
    near = (
        (face_east * value_next + face_west * value_before)
        + (face_north * north + face_south * south)
        + (face_up * up + face_down * down)
    )
    return (1.0 - relax_weight) * value + scale * (source + near)


def sweep(first, last, source_of, value_ref, result_ref, faces_of):
    def one(plane, carried):
        before, value, face_west = carried
        value_next = value_ref[plane + 1]
        face_east, rest = faces_of(plane)
        result_ref[plane] = smooth_plane(
            value, value_next, before, (face_east, face_west, *rest), source_of(plane)
        )
        return value, value_next, face_east

    return one


def assemble(refs, slab_refs, ext_refs, sems, arrays):
    copies = []
    for array in arrays:
        ref, ext, width = refs[array], ext_refs[array], WIDTHS[array]
        extent_x, extent_y = ref.shape[0], ref.shape[1]
        rows = pl.ds(TILE, extent_y)
        start = sum(WIDTHS[:array])
        moves = [
            (ref, ext.at[pl.ds(REACH, extent_x), rows]),
            (slab_refs[0].at[pl.ds(start, width)], ext.at[pl.ds(REACH - width, width), rows]),
            (slab_refs[1].at[pl.ds(start, width)], ext.at[pl.ds(REACH + extent_x, width), rows]),
        ]
        for source, target in moves:
            copy = pltpu.make_async_copy(source, target, sems.at[len(copies)])
            copy.start()
            copies.append(copy)
    return copies


def clear_rims(ext_refs, extent_x, extent_y, arrays):
    for array in arrays:
        ext = ext_refs[array]
        planes = ext.shape[0]
        zeros = jnp.zeros((planes, TILE, LANES), jnp.float32)
        ext[:, 0:TILE, :] = zeros
        ext[:, TILE + extent_y : 2 * TILE + extent_y, :] = zeros
        width = WIDTHS[array]
        for plane in range(REACH - width):
            for side in (plane, planes - 1 - plane):
                ext[side, TILE : TILE + extent_y, :] = jnp.zeros((extent_y, LANES), jnp.float32)


def place_strips(low_ref, high_ref, ext_refs, extent_x, extent_y):
    at = 0
    for array, plane, rows in strip_rows(extent_x):
        ext = ext_refs[array]
        ext[plane, TILE - rows : TILE, :] = low_ref[at : at + rows, :]
        ext[plane, TILE + extent_y : TILE + extent_y + rows, :] = high_ref[at : at + rows, :]
        at += rows


def before_kernel(
    index_ref, cond_in, source_in, value_in, slab_low, slab_high, strip_low, strip_high,
    row_ref, value_out, cond_ext, source_ext, value_ext, other, face_x, face_n, face_s, face_u,
    face_d, scales, sems,
):
    extent_x, extent_y = cond_in.shape[0], cond_in.shape[1]
    planes = extent_x + 2 * REACH
    exts = (cond_ext, source_ext, value_ext)
    copies = assemble(
        (cond_in, source_in, value_in), (slab_low, slab_high), exts, sems, (0, 1, 2)
    )
    clear_rims(exts, extent_x, extent_y, (0, 1, 2))
    place_strips(strip_low, strip_high, exts, extent_x, extent_y)
    for copy in copies:
        copy.wait()
    shape = (extent_y + 2 * TILE, LANES)
    lane = lax.broadcasted_iota(jnp.int32, shape, 1)

    def first(plane, carried):
        before, value, face_west = carried
        value_next = value_ext[plane + 1]
        made = coefficients(cond_ext[plane], cond_ext[plane + 1], face_west, lane)
        for ref, part in zip((face_x, face_n, face_s, face_u, face_d, scales), made):
            ref[plane] = part
        other[plane] = smooth_plane(
            value, value_next, before, (made[0], face_west, *made[1:]), source_ext[plane]
        )
        return value, value_next, made[0]

    face_first = 0.5 * (cond_ext[0] + cond_ext[1])
    lax.fori_loop(1, planes - 1, first, (value_ext[0], value_ext[1], face_first))

    def repeat(low, value_ref, result_ref, shift):
        def one(plane, carried):
            before, value, face_west = carried
            value_next = value_ref[plane + 1]
            face_east = face_x[plane]
            faces = (
                face_east, face_west, face_n[plane], face_s[plane], face_u[plane], face_d[plane],
                scales[plane],
            )
            result_ref[plane - shift] = smooth_plane(
                value, value_next, before, faces, source_ext[plane]
            )
            return value, value_next, face_east

        lax.fori_loop(
            low, planes - low, one, (value_ref[low - 1], value_ref[low], face_x[low - 1])
        )

    repeat(2, other, value_ext, 0)
    repeat(3, value_ext, value_out, NU)

    inner = slice(TILE, TILE + extent_y)
    low_x, high_x = REACH, REACH + extent_x - 1

    def out_x(plane):
        return value_out[plane - NU, inner, :]

    east = face_x[high_x, inner, :]
    west = face_x[low_x - 1, inner, :]
    net = east * (out_x(high_x + 1) - out_x(high_x)) + west * (out_x(low_x - 1) - out_x(low_x))
    edge_low, edge_high = slice(0, 2 * TILE), slice(extent_y, extent_y + 2 * TILE)
    zero = jnp.zeros((extent_y, LANES), jnp.float32)
    zero_edge = jnp.zeros((2 * TILE, LANES), jnp.float32)

    def along(plane, carried):
        sources, flow_low, flow_high, face_low, face_high = carried
        sources = sources + source_ext[plane, inner, :]
        value = value_out[plane - NU, edge_low, :]
        face = face_n[plane, edge_low, :]
        flow_low = flow_low + face * (plane_rolls(value, 0)[0] - value)
        face_low = face_low + face
        value = value_out[plane - NU, edge_high, :]
        face = face_n[plane, edge_high, :]
        flow_high = flow_high + face * (plane_rolls(value, 0)[0] - value)
        face_high = face_high + face
        return sources, flow_low, flow_high, face_low, face_high

    sources, flow_low, flow_high, face_low, face_high = lax.fori_loop(
        low_x, high_x + 1, along, (zero, zero_edge, zero_edge, zero_edge, zero_edge)
    )
    edge_row = lax.broadcasted_iota(jnp.int32, zero_edge.shape, 0) == TILE - 1

    def whole(values):
        return jnp.sum(jnp.sum(values, axis=0, keepdims=True), axis=1, keepdims=True)

    def face_sum(values):
        return whole(jnp.where(edge_row, values, 0.0))

    flow_north, flow_south = face_sum(face_high), face_sum(face_low)
    flow_east, flow_west = whole(east), whole(west)
    residual = whole(sources + net) + face_sum(flow_high) - face_sum(flow_low)
    diag = flow_east + flow_west + flow_north + flow_south
    own = lax.broadcasted_iota(jnp.int32, row_ref.shape, 1)
    count = LANES // 4
    place = own - index_ref[1]
    row_ref[...] = jnp.where(
        place == 0,
        residual,
        jnp.where(
            place == count,
            diag,
            jnp.where(
                place == 2 * count, flow_east, jnp.where(place == 3 * count, flow_north, 0.0)
            ),
        ),
    )


def total(values):
    folded = values[0:8] + values[8:16] + values[16:24] + values[24:32]
    return jnp.sum(jnp.sum(folded, axis=1, keepdims=True), axis=0, keepdims=True)


def shifted(values):
    return (
        pltpu.roll(values, 31, 0),
        pltpu.roll(values, 1, 0),
        pltpu.roll(values, 127, 1),
        pltpu.roll(values, 1, 1),
    )


def coarse_solve(packed, count_x, count_y):
    row = lax.broadcasted_iota(jnp.int32, packed.shape, 0)
    lane = lax.broadcasted_iota(jnp.int32, packed.shape, 1)
    inside = lane < 32
    start = jnp.where(inside, packed, 0.0)
    diag = jnp.where(inside, pltpu.roll(packed, 96, 1), 0.0)
    east = jnp.where(inside & (row < count_x - 1), pltpu.roll(packed, 64, 1), 0.0)
    north = jnp.where(lane < count_y - 1, pltpu.roll(packed, 32, 1), 0.0)
    west = pltpu.roll(east, 1, 0)
    south = pltpu.roll(north, 1, 1)

    def iterate_once(counter, carried):
        estimate, remainder, search, ahead_x, behind_x, ahead_y, behind_y, norm_now = carried
        product = (
            diag * search
            - (east * ahead_x + west * behind_x)
            - (north * ahead_y + south * behind_y)
        )
        alpha_step = norm_now / total(search * product)
        estimate = estimate + alpha_step * search
        remainder = remainder - alpha_step * product
        moved = shifted(remainder)
        norm_next = total(remainder * remainder)
        beta = norm_next / norm_now
        search = remainder + beta * search
        around = [
            m + beta * a for m, a in zip(moved, (ahead_x, behind_x, ahead_y, behind_y))
        ]
        return (estimate, remainder, search, *around, norm_next)

    state = (jnp.zeros_like(start), start, start, *shifted(start), total(start * start))
    return lax.fori_loop(0, CG_ITERS, iterate_once, state)[0]


def after_kernel(
    counts, index_ref, packed_ref, cond_in, source_in, slab_low, slab_high, strip_low, strip_high, value_in,
    out_ref, cond_ext, source_ext, value_ext, other, face_x, face_n, face_s, face_u, face_d,
    scales, sems,
):
    extent_x, extent_y = cond_in.shape[0], cond_in.shape[1]
    planes = extent_x + 2 * REACH
    exts = (cond_ext, source_ext)
    copies = assemble((cond_in, source_in), (slab_low, slab_high), exts, sems, (0, 1))
    copy = pltpu.make_async_copy(value_in, value_ext.at[pl.ds(NU, planes - 2 * NU)], sems.at[6])
    copy.start()
    copies.append(copy)
    estimate = coarse_solve(packed_ref[...], *counts)
    clear_rims(exts, extent_x, extent_y, (0, 1))
    at = 0
    for array, plane, rows in strip_rows(extent_x):
        if array < 2:
            ext = exts[array]
            ext[plane, TILE - rows : TILE, :] = strip_low[at : at + rows, :]
            ext[plane, TILE + extent_y : TILE + extent_y + rows, :] = strip_high[at : at + rows, :]
        at += rows
    shape = (extent_y + 2 * TILE, LANES)
    row = lax.broadcasted_iota(jnp.int32, shape, 0)
    lane = lax.broadcasted_iota(jnp.int32, shape, 1)
    brick_row = lax.broadcasted_iota(jnp.int32, estimate.shape, 0)
    brick_lane = lax.broadcasted_iota(jnp.int32, estimate.shape, 1)

    def share(step_x, step_y):
        mine = (brick_row == index_ref[0] + step_x) & (brick_lane == index_ref[1] + step_y)
        return total(jnp.where(mine, estimate, 0.0))

    def column(step_x):
        low, own, high = (share(step_x, step) for step in (-1, 0, 1))
        return jnp.where(row < TILE, low, jnp.where(row < TILE + extent_y, own, high))

    lifts = [column(step) for step in (-1, 0, 1)]
    for copy in copies:
        copy.wait()

    def lift(low, high, amount):
        def one(plane, carried):
            inside = cond_ext[plane] > 0
            value_ext[plane] = value_ext[plane] + jnp.where(inside, amount, 0.0)
            return carried

        lax.fori_loop(low, high, one, 0)

    lift(NU, REACH, lifts[0])
    lift(REACH, REACH + extent_x, lifts[1])
    lift(REACH + extent_x, planes - NU, lifts[2])

    def first(plane, carried):
        before, value, face_west = carried
        value_next = value_ext[plane + 1]
        made = coefficients(cond_ext[plane], cond_ext[plane + 1], face_west, lane)
        for ref, part in zip((face_x, face_n, face_s, face_u, face_d, scales), made):
            ref[plane] = part
        other[plane] = smooth_plane(
            value, value_next, before, (made[0], face_west, *made[1:]), source_ext[plane]
        )
        return value, value_next, made[0]

    low = NU + 1
    face_first = 0.5 * (cond_ext[low - 1] + cond_ext[low])
    face_x[low - 1] = face_first
    lax.fori_loop(low, planes - low, first, (value_ext[low - 1], value_ext[low], face_first))

    def repeat(low, value_ref, store):
        def one(plane, carried):
            before, value, face_west = carried
            value_next = value_ref[plane + 1]
            face_east = face_x[plane]
            faces = (
                face_east, face_west, face_n[plane], face_s[plane], face_u[plane], face_d[plane],
                scales[plane],
            )
            store(plane, smooth_plane(value, value_next, before, faces, source_ext[plane]))
            return value, value_next, face_east

        lax.fori_loop(
            low, planes - low, one, (value_ref[low - 1], value_ref[low], face_x[low - 1])
        )

    def keep(plane, value):
        value_ext[plane] = value

    def finish(plane, value):
        out_ref[plane - REACH] = value[TILE : TILE + extent_y]

    repeat(NU + 2, other, keep)
    repeat(NU + 3, value_ext, finish)


def spread(row, axis):
    count = lax.axis_size(axis)
    blocks = jnp.broadcast_to(row, (count, row.shape[1]))
    return lax.all_to_all(blocks, axis, 0, 0, tiled=True)


def body(conductivity, source, initial):
    arrays = (conductivity, source, initial)
    extent_x, extent_y = conductivity.shape[:2]
    count_x, count_y = lax.axis_size("gx"), lax.axis_size("gy")
    index = jnp.stack([lax.axis_index("gx"), lax.axis_index("gy")]).astype(jnp.int32)
    tails = jnp.concatenate([a[extent_x - w :] for a, w in zip(arrays, WIDTHS)], 0)
    heads = jnp.concatenate([a[:w] for a, w in zip(arrays, WIDTHS)], 0)
    slabs = (
        lax.ppermute(tails, "gx", ring_pairs(count_x, 1)),
        lax.ppermute(heads, "gx", ring_pairs(count_x, -1)),
    )
    up, down = pack_strips(arrays, slabs)
    strips = (
        lax.ppermute(up, "gy", ring_pairs(count_y, 1)),
        lax.ppermute(down, "gy", ring_pairs(count_y, -1)),
    )
    planes, rows = extent_x + 2 * REACH, extent_y + 2 * TILE
    scratch = [pltpu.VMEM((planes, rows, LANES), jnp.float32)] * 10
    smem = pl.BlockSpec(memory_space=pltpu.SMEM)
    vmem = pl.BlockSpec(memory_space=pltpu.VMEM)
    leave = pl.BlockSpec(memory_space=pl.ANY)
    row, smoothed = pl.pallas_call(
        before_kernel,
        in_specs=[smem] + [leave] * 5 + [vmem] * 2,
        out_specs=[vmem, vmem],
        out_shape=[
            jax.ShapeDtypeStruct((1, LANES), jnp.float32),
            jax.ShapeDtypeStruct((planes - 2 * NU, rows, LANES), jnp.float32),
        ],
        scratch_shapes=scratch + [pltpu.SemaphoreType.DMA((9,))],
        name="smooth_before",
    )(index, *arrays, *slabs, *strips)
    row = jnp.sum(spread(row, "gy"), axis=0, keepdims=True)
    packed = spread(row, "gx")
    packed = jnp.pad(packed, ((0, LANES // 4 - count_x), (0, 0)))
    return pl.pallas_call(
        functools.partial(after_kernel, (count_x, count_y)),
        in_specs=[smem, vmem] + [leave] * 4 + [vmem] * 2 + [leave],
        out_specs=vmem,
        out_shape=jax.ShapeDtypeStruct(conductivity.shape, jnp.float32),
        scratch_shapes=scratch + [pltpu.SemaphoreType.DMA((7,))],
        name="smooth_after",
    )(index, packed, conductivity, source, *slabs, *strips, smoothed)


def solution(mesh):
    return jax.shard_map(
        body,
        mesh=mesh,
        in_specs=(P("gx", "gy", None), P("gx", "gy", None), P("gx", "gy", None)),
        out_specs=P("gx", "gy", None),
        check_vma=False,
    )
```

time: 312 us -> 135 us (0.43)
  the two profiles are of different devices: /device:TPU:36 before, /device:TPU:1 now
where the time goes in v1:
time: 135 us
  blocking collectives  63 us (47%)
  Pallas kernels  39.3 us (29%)
  starting transfers between devices  20.9 us (15%)
  waiting for transfers between devices  6.97 us (5%)
  local copies, waits for them, and re-layouts  4.15 us (3%)
    all_to_all x2, blocking collectives, spread(): return lax.all_to_all(blocks, axis, 0, 0, tiled=True)  63 us
    pallas_call x1, Pallas kernels, body(): pl.pallas_call(functools.partial(after_kernel, (count_x, count_y)), in_sp...  19.8 us
    pallas_call x1, Pallas kernels, body(): pl.pallas_call(before_kernel, in_specs=[smem] + [leave] * 5 + [vmem] * 2,...  17.2 us
    ppermute x1, starting transfers between devices, body(): lax.ppermute(down, 'gy', ring_pairs(count_y, -1))  8.48 us
    ppermute x1, starting transfers between devices, body(): lax.ppermute(up, 'gy', ring_pairs(count_y, 1))  6.75 us
    ppermute x1, starting transfers between devices, body(): lax.ppermute(tails, 'gx', ring_pairs(count_x, 1))  4.38 us
    ppermute x1, waiting for transfers between devices, body(): lax.ppermute(heads, 'gx', ring_pairs(count_x, -1))  4.03 us
  transfers between devices with their start and end apart: 4, of which 3 were waited for; matrix products, arithmetic and copies ran while one was open for 0% of the time, Pallas kernels for 0%

profile of v1, /device:TPU:1, one launch (start us, length us, event | category | flops | bytes accessed | tf_op | source)
XLA Modules:
  0.0 135.0 jit_solution(14745005768645372145)
XLA Ops:
  0.0 0.9 fusion.1
  0.9 1.1 fusion
  2.0 4.4 %collective-permute-start = (f32[17,32,128]{2,1,0:T(8,128)S(1)}, f32[17,32,128]{2,1,0:T(8,128)S(1)}, u32[]{:S(2)}, u32[]{:S(2)}) collective-permute-start(f32[17,32,128]{2,1,0:T(8,128)S(1)} %pad_maximum_fusion), channel_id=1, source_target_pairs={{0,32},{32,64},{64,96},{96,128},{128,160},{160,192},{192,224},{224... | collective-permute-start | bytes 835592 | tf_op jit(solution)/shard_map/ppermute | solution.py:424
  6.5 1.3 collective-permute-start.1
  7.8 2.1 %collective-permute-done.refs_6_.refs_8_.slab_low = f32[17,32,128]{2,1,0:T(8,128)S(1)} collective-permute-done((f32[17,32,128]{2,1,0:T(8,128)S(1)}, f32[17,32,128]{2,1,0:T(8,128)S(1)}, u32[]{:S(2)}, u32[]{:S(2)}) %collective-permute-start) | collective-permute-done | bytes 278560 | tf_op jit(solution)/shard_map/ppermute | solution.py:424
  9.9 0.0 copy-start
  9.9 4.0 %collective-permute-done.1.refs_7_.refs_9_.slab_high = f32[17,32,128]{2,1,0:T(8,128)S(1)} collective-permute-done((f32[17,32,128]{2,1,0:T(8,128)S(1)}, f32[17,32,128]{2,1,0:T(8,128)S(1)}, u32[]{:S(2)}, u32[]{:S(2)}) %collective-permute-start.1) | collective-permute-done | bytes 278560 | tf_op jit(solution)/shard_map/ppermute | solution.py:425
  13.9 0.0 copy-done
  13.9 0.0 copy-start.1
  13.9 0.7 copy-done.1
  14.7 2.2 %pack_strips.1 = (f32[624,128]{1,0:T(8,128)}, f32[624,128]{1,0:T(8,128)}) custom-call(f32[32,32,128]{2,1,0:T(8,128)} %cond_in.3, f32[32,32,128]{2,1,0:T(8,128)} %source_in.3, f32[32,32,128]{2,1,0:T(8,128)} %value_in.1, f32[32,32,128]{2,1,0:T(8,128)} %cond_in.3, f32[32,32,128]{2,1,0:T(8,128)} %source_in.3, f32[32,32,128]{2,1,0:T(8,128)} %value_in.1, ...), custom_call_target="tpu_custom_call" | custom-call | tf_op jit(solution)/shard_map/pack_strips/pallas_call | solution.py:65
  16.9 6.8 %collective-permute-start.2 = (f32[624,128]{1,0:T(8,128)}, f32[624,128]{1,0:T(8,128)S(1)}, u32[]{:S(2)}, u32[]{:S(2)}) collective-permute-start(f32[624,128]{1,0:T(8,128)} %get-tuple-element.9), channel_id=1, source_target_pairs={{0,1},{1,2},{2,3},{3,4},{4,5},{5,6},{6,7},{7,8},{8,9},{9,10},{10,1... | collective-permute-start | bytes 958472 | tf_op jit(solution)/shard_map/ppermute | solution.py:429
  23.6 8.5 %collective-permute-start.3 = (f32[624,128]{1,0:T(8,128)}, f32[624,128]{1,0:T(8,128)S(1)}, u32[]{:S(2)}, u32[]{:S(2)}) collective-permute-start(f32[624,128]{1,0:T(8,128)} %get-tuple-element.10), channel_id=1, source_target_pairs={{1,0},{2,1},{3,2},{4,3},{5,4},{6,5},{7,6},{8,7},{9,8},{10,9},{11,1... | collective-permute-start | bytes 958472 | tf_op jit(solution)/shard_map/ppermute | solution.py:430
  32.1 0.6 pad_add_fusion.index_ref
  32.8 0.0 collective-permute-done.2.strip_low
  32.8 0.8 collective-permute-done.3.strip_high
  33.6 0.0 copy-done.2
  33.6 0.7 copy-done.3
  34.3 17.2 %smooth_before.1 = (f32[1,128]{1,0:T(1,128)}, f32[38,48,128]{2,1,0:T(8,128)}) custom-call(s32[2]{0:T(128)} %pad_add_fusion.index_ref, f32[32,32,128]{2,1,0:T(8,128)} %cond_in.3, f32[32,32,128]{2,1,0:T(8,128)} %source_in.3, f32[32,32,128]{2,1,0:T(8,128)} %value_in.1, f32[17,32,128]{2,1,0:T(8,128)} %copy-done, f32[17,32,128]{2,1,0:T(8,128)} %copy-done.1, ...), custom_call_target="tpu_custom_call" | custom-call | tf_op jit(solution)/shard_map/smooth_before/pallas_call | solution.py:437
  51.5 0.0 copy-start.4
  51.5 0.6 copy-done.4
  52.2 13.8 %all_to_all.14 = f32[32,1,128]{2,1,0:T(1,128)S(1)} all-to-all(f32[32,1,128]{2,1,0:T(1,128)S(1)} %broadcast_in_dim.4), channel_id=1, replica_groups=mesh['gx'=32,'gy'=32] {'gy'}, dimensions={0} | all-to-all | bytes 32768 | tf_op jit(solution)/shard_map/all_to_all | solution.py:413
  66.0 49.2 %all_to_all.15 = f32[32,1,128]{2,1,0:T(1,128)} all-to-all(f32[32,1,128]{2,1,0:T(1,128)S(1)} %broadcast_in_dim.5), channel_id=1, replica_groups=mesh['gx'=32,'gy'=32] {'gx'}, dimensions={0} | all-to-all | bytes 32768 | tf_op jit(solution)/shard_map/all_to_all | solution.py:413
  115.2 19.8 %smooth_after.1 = f32[32,32,128]{2,1,0:T(8,128)} custom-call(s32[2]{0:T(128)} %pad_add_fusion.index_ref, f32[32,128]{1,0:T(8,128)} %bitcast.5, f32[32,32,128]{2,1,0:T(8,128)} %cond_in.3, f32[32,32,128]{2,1,0:T(8,128)} %source_in.3, f32[17,32,128]{2,1,0:T(8,128)} %copy-done, f32[17,32,128]{2,1,0:T(8,128)} %copy-done.1, f32[624,128]{1,0:T(8,128)} %copy-done.2, ...), custom_call_target="tpu_custom_call" | custom-call | tf_op jit(solution)/shard_map/smooth_after/pallas_call | solution.py:451
  (7 shorter events, 0.1 us)
Async XLA Ops:
  2.0 7.8 %collective-permute-start = (f32[17,32,128]{2,1,0:T(8,128)S(1)}, f32[17,32,128]{2,1,0:T(8,128)S(1)}, u32[]{:S(2)}, u32[]{:S(2)}) collective-permute-start(f32[17,32,128]{2,1,0:T(8,128)S(1)} %pad_maximum_fusion), channel_id=1, source_target_pairs={{0,32},{32,64},{64,96},{96,128},{128,160},{160,192},{192,224},{224... | collective-permute-start | bytes 835592 | tf_op jit(solution)/shard_map/ppermute | solution.py:424
  6.5 7.5 %collective-permute-start.1 = (f32[17,32,128]{2,1,0:T(8,128)S(1)}, f32[17,32,128]{2,1,0:T(8,128)S(1)}, u32[]{:S(2)}, u32[]{:S(2)}) collective-permute-start(f32[17,32,128]{2,1,0:T(8,128)S(1)} %pad_maximum_fusion.1), channel_id=1, source_target_pairs={{32,0},{64,32},{96,64},{128,96},{160,128},{192,160},{224,192},{256... | collective-permute-start | bytes 835592 | tf_op jit(solution)/shard_map/ppermute | solution.py:425
  9.9 4.0 %copy-start = (f32[17,32,128]{2,1,0:T(8,128)}, f32[17,32,128]{2,1,0:T(8,128)S(1)}, u32[]{:S(2)}) copy-start(f32[17,32,128]{2,1,0:T(8,128)S(1)} %collective-permute-done.refs_6_.refs_8_.slab_low) | copy-start | bytes 835588
  13.9 0.7 copy-start.1
  16.9 15.9 %collective-permute-start.2 = (f32[624,128]{1,0:T(8,128)}, f32[624,128]{1,0:T(8,128)S(1)}, u32[]{:S(2)}, u32[]{:S(2)}) collective-permute-start(f32[624,128]{1,0:T(8,128)} %get-tuple-element.9), channel_id=1, source_target_pairs={{0,1},{1,2},{2,3},{3,4},{4,5},{5,6},{6,7},{7,8},{8,9},{9,10},{10,1... | collective-permute-start | bytes 958472 | tf_op jit(solution)/shard_map/ppermute | solution.py:429
  23.6 9.9 %collective-permute-start.3 = (f32[624,128]{1,0:T(8,128)}, f32[624,128]{1,0:T(8,128)S(1)}, u32[]{:S(2)}, u32[]{:S(2)}) collective-permute-start(f32[624,128]{1,0:T(8,128)} %get-tuple-element.10), channel_id=1, source_target_pairs={{1,0},{2,1},{3,2},{4,3},{5,4},{6,5},{7,6},{8,7},{9,8},{10,9},{11,1... | collective-permute-start | bytes 958472 | tf_op jit(solution)/shard_map/ppermute | solution.py:430
  32.8 0.8 copy-start.2
  33.6 0.7 copy-start.3
  51.5 0.7 copy-start.4

commit v2 on v0

v2 whole, which is shorter than its diff:
```python
import jax
import jax.numpy as jnp
from jax import lax
from jax.experimental import pallas as pl
from jax.experimental.pallas import tpu as pltpu
from jax.sharding import PartitionSpec as P

NU = 3
CG_ITERS = 32


relax_weight = 0.8
REACH = 2 * NU
WIDTHS = (REACH, REACH - 1, REACH)
LANES = 128
TILE = 8
SIDE = 32


def ring_pairs(count, step):
    return [(i, i + step) for i in range(count) if 0 <= i + step < count]


def own_rows():
    return [(array, row) for array, width in enumerate(WIDTHS) for row in range(width)]


def corner_rows(extent_x):
    rows = []
    for array, width in enumerate(WIDTHS):
        for beyond in range(1, width):
            for plane in (REACH - beyond, REACH + extent_x - 1 + beyond):
                rows.append((array, plane, width - beyond))
    return rows


def slab_plane(array, plane, extent_x):
    start = sum(WIDTHS[:array])
    if plane < REACH:
        return 0, start + plane - (REACH - WIDTHS[array])
    return 1, start + plane - (REACH + extent_x)


def vmem_array(shape):
    return pltpu.VMEM(shape, jnp.float32)


def vmem_result(shape):
    return vmem_array(shape)


def in_vmem(array):
    return pltpu.with_memory_space_constraint(array, pltpu.VMEM)


vmem = pl.BlockSpec(memory_space=pltpu.VMEM)
leave = pl.BlockSpec(memory_space=pl.ANY)
limits = pltpu.CompilerParams(vmem_limit_bytes=24 * 2**20)


def strip_length(extent_x):
    own = extent_x * len(own_rows())
    return own, own + sum(rows for _, _, rows in corner_rows(extent_x))


def pack_own(arrays):
    extent_x, extent_y = arrays[0].shape[:2]
    last = extent_y // TILE - 1
    length = strip_length(extent_x)[0]

    def kernel(*refs):
        low_refs, high_refs, up_ref, down_ref = refs[0:3], refs[3:6], refs[6], refs[7]
        for k, (array, row) in enumerate(own_rows()):
            rows = slice(k * extent_x, (k + 1) * extent_x)
            up_ref[rows, :] = high_refs[array][:, TILE - WIDTHS[array] + row, :]
            down_ref[rows, :] = low_refs[array][:, row, :]

    def edge(array, block):
        return pl.BlockSpec((array.shape[0], TILE, LANES), lambda i: (0, block, 0))

    return pl.pallas_call(
        kernel,
        grid=(1,),
        in_specs=[edge(a, 0) for a in arrays] + [edge(a, last) for a in arrays],
        out_specs=[vmem] * 2,
        out_shape=[vmem_result((length, LANES))] * 2,
        compiler_params=limits,
        name="pack_own",
    )(*arrays, *arrays)


def pack_corners(strips, slabs, extent_x):
    own, length = strip_length(extent_x)

    def kernel(own_up, own_down, low_ref, high_ref, up_ref, down_ref):
        up_ref[0:own, :] = own_up[...]
        down_ref[0:own, :] = own_down[...]
        at = own
        for array, plane, rows in corner_rows(extent_x):
            side, where = slab_plane(array, plane, extent_x)
            slab = (low_ref, high_ref)[side]
            last = slab.shape[1]
            up_ref[at : at + rows, :] = slab[where, last - rows : last, :]
            down_ref[at : at + rows, :] = slab[where, 0:rows, :]
            at += rows

    return pl.pallas_call(
        kernel,
        in_specs=[vmem] * 4,
        out_specs=[vmem] * 2,
        out_shape=[vmem_result((length, LANES))] * 2,
        compiler_params=limits,
        name="pack_corners",
    )(*map(in_vmem, strips), *map(in_vmem, slabs))


def plane_rolls(values, axis):
    return pltpu.roll(values, values.shape[axis] - 1, axis), pltpu.roll(values, 1, axis)


def coefficients(cond, cond_next, face_west):
    lane = lax.broadcasted_iota(jnp.int32, cond.shape, 1)
    cond_up, cond_down = plane_rolls(cond, 1)
    face_east = 0.5 * (cond + cond_next)
    face_north = 0.5 * (cond + plane_rolls(cond, 0)[0])
    face_south = plane_rolls(face_north, 0)[1]
    face_up = jnp.where(lane < LANES - 1, 0.5 * (cond + cond_up), 0.0)
    face_down = jnp.where(lane > 0, 0.5 * (cond + cond_down), 0.0)
    diagonal = (face_east + face_west) + (face_north + face_south) + (face_up + face_down)
    scale = jnp.where(cond > 0, relax_weight / diagonal, 0.0)
    return face_east, face_north, face_south, face_up, face_down, scale


def prepare(first, size, cond_ref, face_refs, face_west):
    limit = cond_ref.shape[0] - 1
    for k in range(size):
        plane = first + k
        made = coefficients(cond_ref[plane], cond_ref[jnp.minimum(plane + 1, limit)], face_west)
        for ref, part in zip(face_refs, made):
            ref[plane] = part
        face_west = made[0]
    return face_west


def sweep(low, count, size, value_ref, source_ref, face_refs, term_ref, store):
    face_x, face_n, face_s, face_u, face_d, scales = face_refs
    limit = value_ref.shape[0] - 1

    def make_terms(planes, rolled):
        for plane, (up, down) in zip(planes, rolled):
            term_ref[plane] = face_u[plane] * up + face_d[plane] * down

    def block(index, carried):
        before, value, face_west = carried
        base = low + index * size
        ahead = [jnp.minimum(base + size + k, limit) for k in range(size)]
        rolled = [plane_rolls(value_ref[plane], 1) for plane in ahead]
        for k in range(size):
            plane = base + k
            value_next = value_ref[plane + 1]
            face_east = face_x[plane]
            north, south = plane_rolls(value, 0)
            near = (face_east * value_next + face_west * before) + (
                face_n[plane] * north + face_s[plane] * south
            )
            near = (near + term_ref[plane]) + source_ref[plane]
            store(index, k, plane, (1.0 - relax_weight) * value + scales[plane] * near)
            before, value, face_west = value, value_next, face_east
        make_terms(ahead, rolled)
        return before, value, face_west

    planes = [low + k for k in range(size)]
    make_terms(planes, [plane_rolls(value_ref[plane], 1) for plane in planes])
    start = (value_ref[low - 1], value_ref[low], face_x[low - 1])
    lax.fori_loop(0, count // size, block, start)


def keep_in(ref):
    def store(index, k, plane, value):
        ref[plane] = value

    return store


def start_copies(pairs, sems):
    copies = [pltpu.make_async_copy(a, b, sems.at[k]) for k, (a, b) in enumerate(pairs)]
    for copy in copies:
        copy.start()
    return copies


def own_part(ext, extent_x, extent_y):
    return ext.at[pl.ds(REACH, extent_x), pl.ds(TILE, extent_y)]


def place_halos(ext_refs, slab_refs, strip_refs, extent_x, extent_y, arrays):
    inner = slice(TILE, TILE + extent_y)
    for array in arrays:
        ext, width = ext_refs[array], WIDTHS[array]
        planes = ext.shape[0]
        zeros = jnp.zeros((planes, TILE, LANES), jnp.float32)
        ext[:, 0:TILE, :] = zeros
        ext[:, TILE + extent_y : 2 * TILE + extent_y, :] = zeros
        for plane in range(REACH - width):
            for side in (plane, planes - 1 - plane):
                ext[side, inner, :] = jnp.zeros((extent_y, LANES), jnp.float32)
        start = sum(WIDTHS[:array])
        part = slice(start, start + width)
        ext[REACH - width : REACH, inner, :] = slab_refs[0][part]
        ext[REACH + extent_x : REACH + extent_x + width, inner, :] = slab_refs[1][part]
    low_ref, high_ref = strip_refs
    for k, (array, row) in enumerate(own_rows()):
        if array in arrays:
            ext, rows = ext_refs[array], slice(k * extent_x, (k + 1) * extent_x)
            own = slice(REACH, REACH + extent_x)
            ext[own, TILE - WIDTHS[array] + row, :] = low_ref[rows, :]
            ext[own, TILE + extent_y + row, :] = high_ref[rows, :]
    at = strip_length(extent_x)[0]
    for array, plane, rows in corner_rows(extent_x):
        if array in arrays:
            ext = ext_refs[array]
            ext[plane, TILE - rows : TILE, :] = low_ref[at : at + rows, :]
            ext[plane, TILE + extent_y : TILE + extent_y + rows, :] = high_ref[at : at + rows, :]
        at += rows


def before_kernel(
    cond_in, source_in, value_in, slab_low, slab_high, strip_low, strip_high, row_ref, value_out,
    cond_ext, source_ext, value_ext, other, term, face_x, face_n, face_s, face_u, face_d, scales,
    sems, out_sem,
):
    extent_x, extent_y = cond_in.shape[0], cond_in.shape[1]
    planes = extent_x + 2 * REACH
    exts = (cond_ext, source_ext, value_ext)
    face_refs = (face_x, face_n, face_s, face_u, face_d, scales)
    pairs = [
        (ref, own_part(ext, extent_x, extent_y))
        for ref, ext in zip((cond_in, source_in, value_in), exts)
    ]
    copies = start_copies(pairs, sems)
    place_halos(
        exts, (slab_low, slab_high), (strip_low, strip_high), extent_x, extent_y, (0, 1, 2)
    )
    blank = jnp.zeros(cond_ext.shape[1:], jnp.float32)
    other[0] = blank
    other[planes - 1] = blank
    for copy in copies:
        copy.wait()

    def prepare_block(index, face_west):
        return prepare(4 * index, 4, cond_ext, face_refs, face_west)

    lax.fori_loop(0, planes // 4, prepare_block, blank)
    shared = (source_ext, face_refs, term)
    sweep(1, planes - 2, 3, value_ext, *shared, keep_in(other))
    sweep(1, planes - 2, 3, other, *shared, keep_in(value_ext))
    sweep(1, planes - 2, 3, value_ext, *shared, keep_in(other))
    kept = pltpu.make_async_copy(other.at[pl.ds(NU, planes - 2 * NU)], value_out, out_sem)
    kept.start()

    inner = slice(TILE, TILE + extent_y)
    low_x, high_x = REACH, REACH + extent_x - 1
    east = face_x[high_x, inner, :]
    west = face_x[low_x - 1, inner, :]
    net = east * (other[high_x + 1, inner, :] - other[high_x, inner, :]) + west * (
        other[low_x - 1, inner, :] - other[low_x, inner, :]
    )
    edge_low, edge_high = slice(0, 2 * TILE), slice(extent_y, extent_y + 2 * TILE)
    zero = jnp.zeros((extent_y, LANES), jnp.float32)
    zero_edge = jnp.zeros((2 * TILE, LANES), jnp.float32)

    def along(index, carried):
        sources, flow_low, flow_high, face_low, face_high = carried
        for k in range(4):
            plane = low_x + 4 * index + k
            sources = sources + source_ext[plane, inner, :]
            value = other[plane, edge_low, :]
            face = face_n[plane, edge_low, :]
            flow_low = flow_low + face * (plane_rolls(value, 0)[0] - value)
            face_low = face_low + face
            value = other[plane, edge_high, :]
            face = face_n[plane, edge_high, :]
            flow_high = flow_high + face * (plane_rolls(value, 0)[0] - value)
            face_high = face_high + face
        return sources, flow_low, flow_high, face_low, face_high

    sources, flow_low, flow_high, face_low, face_high = lax.fori_loop(
        0, extent_x // 4, along, (zero, zero_edge, zero_edge, zero_edge, zero_edge)
    )
    edge_row = lax.broadcasted_iota(jnp.int32, zero_edge.shape, 0) == TILE - 1

    def whole(values):
        return jnp.sum(jnp.sum(values, axis=0, keepdims=True), axis=1, keepdims=True)

    def face_sum(values):
        return whole(jnp.where(edge_row, values, 0.0))

    flow_north, flow_south = face_sum(face_high), face_sum(face_low)
    flow_east, flow_west = whole(east), whole(west)
    residual = whole(sources + net) + (face_sum(flow_high) - face_sum(flow_low))
    diag = flow_east + flow_west + flow_north + flow_south
    place = lax.broadcasted_iota(jnp.int32, row_ref.shape, 1) - lax.axis_index("gy")
    row = jnp.where(place == 3 * SIDE, flow_north, 0.0)
    row = jnp.where(place == 2 * SIDE, flow_east, row)
    row = jnp.where(place == SIDE, diag, row)
    row_ref[...] = jnp.where(place == 0, residual, row)
    kept.wait()


def total(values):
    return jnp.sum(jnp.sum(values, axis=1, keepdims=True), axis=0, keepdims=True)


def brick_index(shape):
    sublane = lax.broadcasted_iota(jnp.int32, shape, 0)
    lane = lax.broadcasted_iota(jnp.int32, shape, 1)
    return lane // SIDE * TILE + sublane, lane % SIDE


def fold(packed_ref, turn, part):
    lane = lax.broadcasted_iota(jnp.int32, (TILE, LANES), 1)
    folded = jnp.zeros((TILE, LANES), jnp.float32)
    for group in range(LANES // SIDE):
        start = (group + turn) % (SIDE // TILE) * TILE
        rows = packed_ref[start : start + TILE, :]
        shift = SIDE * (group - part) % LANES
        rows = pltpu.roll(rows, shift, 1) if shift else rows
        folded = jnp.where(lane // SIDE == group, rows, folded)
    return folded


def around(values):
    sublane = lax.broadcasted_iota(jnp.int32, values.shape, 0)
    ahead, behind = plane_rolls(values, 0)
    return (
        jnp.where(sublane == TILE - 1, pltpu.roll(ahead, LANES - SIDE, 1), ahead),
        jnp.where(sublane == 0, pltpu.roll(behind, SIDE, 1), behind),
        pltpu.roll(values, LANES - 1, 1),
        pltpu.roll(values, 1, 1),
    )


def coarse_solver(packed_ref, turn, count_x, count_y):
    start, diag, east, north = (fold(packed_ref, turn, part) for part in range(4))
    brick_x, brick_y = brick_index(start.shape)
    east = jnp.where(brick_x < count_x - 1, east, 0.0)
    north = jnp.where(brick_y < count_y - 1, north, 0.0)
    west, south = around(east)[1], around(north)[3]

    def products(remainder, beside):
        image = (
            diag * remainder
            - (east * beside[0] + west * beside[1])
            - (north * beside[2] + south * beside[3])
        )
        return image, around(image), total(remainder * remainder), total(image * remainder)

    def moved(state, alpha, norm, search, image, image_beside):
        estimate, remainder, beside = state
        estimate = estimate + alpha * search
        remainder = remainder - alpha * image
        beside = tuple(b - alpha * i for b, i in zip(beside, image_beside))
        return estimate, remainder, beside, search, image, image_beside, norm, alpha

    beside = around(start)
    image, image_beside, norm, curve = products(start, beside)
    first = moved(
        (jnp.zeros_like(start), start, beside), norm / curve, norm, start, image, image_beside
    )

    def iterate_once(carried):
        estimate, remainder, beside, search, image, image_beside, norm_before, alpha = carried
        new_image, new_beside, norm, curve = products(remainder, beside)
        beta = norm / norm_before
        alpha = norm / (curve - beta * norm / alpha)
        search = remainder + beta * search
        image = new_image + beta * image
        image_beside = tuple(n + beta * i for n, i in zip(new_beside, image_beside))
        return moved(
            (estimate, remainder, beside), alpha, norm, search, image, image_beside
        )

    return first, iterate_once


def after_kernel(turn, counts):
    def kernel(
        packed_ref, cond_in, source_in, value_in, slab_low, slab_high, strip_low, strip_high,
        out_ref, cond_ext, source_ext, value_ext, other, term, face_x, face_n, face_s, face_u,
        face_d, scales, out_part, sems, out_sems,
    ):
        extent_x, extent_y = cond_in.shape[0], cond_in.shape[1]
        planes = extent_x + 2 * REACH
        exts = (cond_ext, source_ext)
        face_refs = (face_x, face_n, face_s, face_u, face_d, scales)
        copies = start_copies(
            [
                (cond_in, own_part(cond_ext, extent_x, extent_y)),
                (source_in, own_part(source_ext, extent_x, extent_y)),
                (value_in, value_ext.at[pl.ds(NU, planes - 2 * NU)]),
            ],
            sems,
        )
        place_halos(
            exts, (slab_low, slab_high), (strip_low, strip_high), extent_x, extent_y, (0, 1)
        )
        state, iterate_once = coarse_solver(packed_ref, turn, *counts)
        low = NU + 1
        pairs = (planes - 2 * low) // 2
        lead = min(6, max(CG_ITERS - 1 - pairs, 0))
        state = lax.fori_loop(0, lead, lambda i, s: iterate_once(s), state)
        for copy in copies:
            copy.wait()
        face_west = 0.5 * (cond_ext[low - 1] + cond_ext[low])
        face_x[low - 1] = face_west

        def both(index, carried):
            face_west = prepare(low + 2 * index, 2, cond_ext, face_refs, carried[1])
            return iterate_once(carried[0]), face_west

        shared = min(pairs, CG_ITERS - 1 - lead)
        state, face_west = lax.fori_loop(0, shared, both, (state, face_west))
        if shared < pairs:
            prepare(low + 2 * shared, 2 * (pairs - shared), cond_ext, face_refs, face_west)
        rest = CG_ITERS - 1 - lead - shared
        state = lax.fori_loop(0, rest, lambda i, s: iterate_once(s), state)
        estimate = state[0]

        brick_x, brick_y = brick_index(estimate.shape)
        step_x = brick_x - lax.axis_index("gx")
        step_y = brick_y - lax.axis_index("gy")
        row = lax.broadcasted_iota(jnp.int32, cond_ext.shape[1:], 0)

        def lift_of(step):
            low, own, high = (
                total(jnp.where((step_x == step) & (step_y == side), estimate, 0.0))
                for side in (-1, 0, 1)
            )
            return jnp.where(row < TILE, low, jnp.where(row < TILE + extent_y, own, high))

        lifts = [lift_of(step) for step in (-1, 0, 1)]

        def lift(plane, amount):
            inside = cond_ext[plane] > 0
            value_ext[plane] = value_ext[plane] + jnp.where(inside, amount, 0.0)

        for k in range(NU):
            lift(NU + k, lifts[0])
            lift(REACH + extent_x + k, lifts[2])

        def lift_block(index, carried):
            for k in range(4):
                lift(REACH + 4 * index + k, lifts[1])
            return carried

        lax.fori_loop(0, extent_x // 4, lift_block, 0)

        shared = (source_ext, face_refs, term)
        sweep(low, planes - 2 * low, 3, value_ext, *shared, keep_in(other))
        sweep(low + 1, planes - 2 * low, 3, other, *shared, keep_in(value_ext))
        size = 4

        def part(index):
            rows = pl.ds(index * size, size)
            return pltpu.make_async_copy(out_part.at[rows], out_ref.at[rows], out_sems.at[index])

        def finish(index, k, plane, value):
            out_part[index * size + k] = value[TILE : TILE + extent_y]
            if k == size - 1:
                part(index).start()

        sweep(REACH, extent_x, size, value_ext, *shared, finish)
        for index in range(extent_x // size):
            part(index).wait()

    return kernel


def spread(rows, axis, order):
    return lax.all_to_all(rows, axis, 0, 0, tiled=True, axis_index_groups=[order])


def body(conductivity, source, initial):
    arrays = (conductivity, source, initial)
    extent_x, extent_y = conductivity.shape[:2]
    count_x, count_y = lax.axis_size("gx"), lax.axis_size("gy")
    tails = jnp.concatenate([a[extent_x - w :] for a, w in zip(arrays, WIDTHS)], 0)
    heads = jnp.concatenate([a[:w] for a, w in zip(arrays, WIDTHS)], 0)
    slabs = (
        lax.ppermute(tails, "gx", ring_pairs(count_x, 1)),
        lax.ppermute(heads, "gx", ring_pairs(count_x, -1)),
    )
    up, down = pack_corners(pack_own(arrays), slabs, extent_x)
    strips = (
        lax.ppermute(up, "gy", ring_pairs(count_y, 1)),
        lax.ppermute(down, "gy", ring_pairs(count_y, -1)),
    )
    halos = [in_vmem(a) for a in (*slabs, *strips)]
    planes, rows = extent_x + 2 * REACH, extent_y + 2 * TILE
    scratch = [vmem_array((planes, rows, LANES))] * 11 + [pltpu.SemaphoreType.DMA((3,))]
    row, smoothed = pl.pallas_call(
        before_kernel,
        in_specs=[leave] * 3 + [vmem] * 4,
        out_specs=[vmem, leave],
        out_shape=[
            jax.ShapeDtypeStruct((count_y, LANES), jnp.float32),
            jax.ShapeDtypeStruct((planes - 2 * NU, rows, LANES), jnp.float32),
        ],
        scratch_shapes=scratch + [pltpu.SemaphoreType.DMA],
        compiler_params=limits,
        name="smooth_before",
    )(*arrays, *halos)
    row = jnp.sum(spread(row, "gy", list(range(count_y))), axis=0, keepdims=True)
    half = count_x // 2
    order = list(range(half, count_x)) + list(range(half))
    packed = spread(jnp.broadcast_to(row, (count_x, LANES)), "gx", order)
    turn = SIDE // TILE // 2
    if count_x != SIDE:
        packed = jnp.pad(jnp.roll(packed, half, 0), ((0, SIDE - count_x), (0, 0)))
        turn = 0
    return pl.pallas_call(
        after_kernel(turn, (count_x, count_y)),
        in_specs=[vmem] + [leave] * 3 + [vmem] * 4,
        out_specs=leave,
        out_shape=jax.ShapeDtypeStruct(conductivity.shape, jnp.float32),
        scratch_shapes=scratch[:-1]
        + [vmem_array(conductivity.shape), scratch[-1], pltpu.SemaphoreType.DMA((extent_x // 4,))],
        compiler_params=limits,
        name="smooth_after",
    )(packed, conductivity, source, smoothed, *halos)


def solution(mesh):
    return jax.shard_map(
        body,
        mesh=mesh,
        in_specs=(P("gx", "gy", None), P("gx", "gy", None), P("gx", "gy", None)),
        out_specs=P("gx", "gy", None),
        check_vma=False,
    )
```

time: 312 us -> 98.6 us (0.32)
  the two profiles are of different devices: /device:TPU:36 before, /device:TPU:1 now
where the time goes in v2:
time: 98.6 us; the launch traced here: 98.2 us
  blocking collectives  49.4 us (50%)
  starting transfers between devices  21 us (21%)
  Pallas kernels  18.4 us (19%)
  waiting for transfers between devices  6.97 us (7%)
  local copies, waits for them, and re-layouts  2.09 us (2%)
    all_to_all x2, blocking collectives, spread(): lax.all_to_all(rows, axis, 0, 0, tiled=True, axis_index_groups=[order])  49.4 us
    pallas_call x1, Pallas kernels, body(): pl.pallas_call(after_kernel(turn, (count_x, count_y)), in_specs=[vmem] +...  9.63 us
    ppermute x1, starting transfers between devices, body(): lax.ppermute(down, 'gy', ring_pairs(count_y, -1))  8.48 us
    pallas_call x1, Pallas kernels, body(): pl.pallas_call(before_kernel, in_specs=[leave] * 3 + [vmem] * 4, out_spec...  8.4 us
    ppermute x1, starting transfers between devices, body(): lax.ppermute(up, 'gy', ring_pairs(count_y, 1))  6.76 us
    ppermute x1, starting transfers between devices, body(): lax.ppermute(tails, 'gx', ring_pairs(count_x, 1))  4.51 us
    ppermute x1, waiting for transfers between devices, body(): lax.ppermute(heads, 'gx', ring_pairs(count_x, -1))  4.03 us
    slice x2, local copies, waits for them, and re-layouts, body(): heads = jnp.concatenate([a[:w] for a, w in zip(arrays, WIDTHS)], 0)  2.06 us
  transfers between devices with their start and end apart: 4, of which 3 were waited for; matrix products, arithmetic and copies ran while one was open for 0% of the time, Pallas kernels for 0%

profile of v2, /device:TPU:1, one launch (start us, length us, event | category | flops | bytes accessed | tf_op | source)
XLA Modules:
  0.0 98.2 jit_solution(16750347671050736071)
XLA Ops:
  0.0 0.9 fusion.1
  0.9 0.0 copy-start.2
  1.0 1.1 %fusion = (f32[6,32,128]{2,1,0:T(8,128)S(1)}, f32[6,32,128]{2,1,0:T(8,128)S(1)}, f32[6,32,128]{2,1,0:T(8,128)S(1)}, f32[6,32,128]{2,1,0:T(8,128)S(1)}) fusion(f32[32,32,128]{2,1,0:T(8,128)} %cond_in.3, f32[32,32,128]{2,1,0:T(8,128)} %value_in.1), kind=kLoop, calls=%fused_computation.2 | loop fusion | bytes 786432 | tf_op jit(solution)/shard_map/slice | solution.py:488
  2.1 0.0 copy-start
  2.1 0.0 copy-start.1
  2.1 4.5 %collective-permute-start = (f32[17,32,128]{2,1,0:T(8,128)S(1)}, f32[17,32,128]{2,1,0:T(8,128)S(1)}, u32[]{:S(2)}, u32[]{:S(2)}) collective-permute-start(f32[17,32,128]{2,1,0:T(8,128)S(1)} %pad_maximum_fusion), channel_id=1, source_target_pairs={{0,32},{32,64},{64,96},{96,128},{128,160},{160,192},{192,224},{224... | collective-permute-start | bytes 835592 | tf_op jit(solution)/shard_map/ppermute | solution.py:490
  6.7 1.3 %collective-permute-start.1 = (f32[17,32,128]{2,1,0:T(8,128)S(1)}, f32[17,32,128]{2,1,0:T(8,128)S(1)}, u32[]{:S(2)}, u32[]{:S(2)}) collective-permute-start(f32[17,32,128]{2,1,0:T(8,128)S(1)} %pad_maximum_fusion.1), channel_id=1, source_target_pairs={{32,0},{64,32},{96,64},{128,96},{160,128},{192,160},{224,192},{256... | collective-permute-start | bytes 835592 | tf_op jit(solution)/shard_map/ppermute | solution.py:491
  8.0 0.0 copy-done.2
  8.0 0.0 copy-done
  8.0 0.0 copy-done.1
  8.0 0.4 pack_own.1
  8.4 1.7 %collective-permute-done.low_ref.slab_low = f32[17,32,128]{2,1,0:T(8,128)S(1)} collective-permute-done((f32[17,32,128]{2,1,0:T(8,128)S(1)}, f32[17,32,128]{2,1,0:T(8,128)S(1)}, u32[]{:S(2)}, u32[]{:S(2)}) %collective-permute-start) | collective-permute-done | bytes 278560 | tf_op jit(solution)/shard_map/ppermute | solution.py:490
  10.1 4.0 %collective-permute-done.1.high_ref.slab_high = f32[17,32,128]{2,1,0:T(8,128)S(1)} collective-permute-done((f32[17,32,128]{2,1,0:T(8,128)S(1)}, f32[17,32,128]{2,1,0:T(8,128)S(1)}, u32[]{:S(2)}, u32[]{:S(2)}) %collective-permute-start.1) | collective-permute-done | bytes 278560 | tf_op jit(solution)/shard_map/ppermute | solution.py:491
  14.1 0.1 pack_corners.1
  14.2 6.8 %collective-permute-start.2 = (f32[624,128]{1,0:T(8,128)S(1)}, f32[624,128]{1,0:T(8,128)S(1)}, u32[]{:S(2)}, u32[]{:S(2)}) collective-permute-start(f32[624,128]{1,0:T(8,128)S(1)} %get-tuple-element.13), channel_id=1, source_target_pairs={{0,1},{1,2},{2,3},{3,4},{4,5},{5,6},{6,7},{7,8},{8,9},{9,10},{10,1... | collective-permute-start | bytes 958472 | tf_op jit(solution)/shard_map/ppermute | solution.py:495
  21.0 8.5 %collective-permute-start.3 = (f32[624,128]{1,0:T(8,128)S(1)}, f32[624,128]{1,0:T(8,128)S(1)}, u32[]{:S(2)}, u32[]{:S(2)}) collective-permute-start(f32[624,128]{1,0:T(8,128)S(1)} %get-tuple-element.14), channel_id=1, source_target_pairs={{1,0},{2,1},{3,2},{4,3},{5,4},{6,5},{7,6},{8,7},{9,8},{10,9},{11,1... | collective-permute-start | bytes 958472 | tf_op jit(solution)/shard_map/ppermute | solution.py:496
  29.5 0.0 collective-permute-done.2.strip_low
  29.5 1.2 %collective-permute-done.3.strip_high = f32[624,128]{1,0:T(8,128)S(1)} collective-permute-done((f32[624,128]{1,0:T(8,128)S(1)}, f32[624,128]{1,0:T(8,128)S(1)}, u32[]{:S(2)}, u32[]{:S(2)}) %collective-permute-start.3) | collective-permute-done | bytes 319520 | tf_op jit(solution)/shard_map/ppermute | solution.py:496
  30.7 8.4 %smooth_before.1 = (f32[32,128]{1,0:T(8,128)S(1)}, f32[38,48,128]{2,1,0:T(8,128)S(1)}) custom-call(f32[32,32,128]{2,1,0:T(8,128)S(1)} %copy-done, f32[32,32,128]{2,1,0:T(8,128)S(1)} %copy-done.1, f32[32,32,128]{2,1,0:T(8,128)S(1)} %copy-done.2, f32[17,32,128]{2,1,0:T(8,128)S(1)} %collective-permute-done.low_ref.slab_low, ...), custom_call_target="tpu_custom_call" | custom-call | tf_op jit(solution)/shard_map/smooth_before/pallas_call | solution.py:501
  39.1 13.8 %all_to_all.17 = f32[32,1,128]{2,1,0:T(1,128)S(1)} all-to-all(f32[32,1,128]{2,1,0:T(1,128)S(1)} %bitcast.5), channel_id=1, replica_groups={{0,1,2,3,4,5,6,7,8,9,10,11,12,13,14,15,16,17,18,19,20,21,22,23,24,25,26..., dimensions={0} | all-to-all | bytes 32768 | tf_op jit(solution)/shard_map/all_to_all | solution.py:480
  52.9 0.1 reduce_sum.9
  52.9 35.6 %all_to_all.18 = f32[32,1,128]{2,1,0:T(1,128)S(1)} all-to-all(f32[32,1,128]{2,1,0:T(1,128)S(1)} %broadcast_in_dim.2), channel_id=1, replica_groups={{512,544,576,608,640,672,704,736,768,800,832,864,896,928,960,992,0,32,6..., dimensions={0} | all-to-all | bytes 32768 | tf_op jit(solution)/shard_map/all_to_all | solution.py:480
  88.5 9.6 %smooth_after.1 = f32[32,32,128]{2,1,0:T(8,128)} custom-call(f32[32,128]{1,0:T(8,128)S(1)} %bitcast.4, f32[32,32,128]{2,1,0:T(8,128)S(1)} %copy-done, f32[32,32,128]{2,1,0:T(8,128)S(1)} %copy-done.1, f32[38,48,128]{2,1,0:T(8,128)S(1)} %get-tuple-element.16.value_in, f32[17,32,128]{2,1,0:T(8,128)S(1)} %collective-permute-done.low_ref.slab_low, ...), custom_call_target="tpu_custom_call" | custom-call | tf_op jit(solution)/shard_map/smooth_after/pallas_call | solution.py:521
  (3 shorter events, 0.1 us)
Async XLA Ops:
  0.9 7.0 %copy-start.2 = (f32[32,32,128]{2,1,0:T(8,128)S(1)}, f32[32,32,128]{2,1,0:T(8,128)}, u32[]{:S(2)}) copy-start(f32[32,32,128]{2,1,0:T(8,128)} %value_in.1) | copy-start | bytes 1572868
  2.1 5.9 %copy-start = (f32[32,32,128]{2,1,0:T(8,128)S(1)}, f32[32,32,128]{2,1,0:T(8,128)}, u32[]{:S(2)}) copy-start(f32[32,32,128]{2,1,0:T(8,128)} %cond_in.3) | copy-start | bytes 1572868
  2.1 5.9 %copy-start.1 = (f32[32,32,128]{2,1,0:T(8,128)S(1)}, f32[32,32,128]{2,1,0:T(8,128)}, u32[]{:S(2)}) copy-start(f32[32,32,128]{2,1,0:T(8,128)} %source_in.3) | copy-start | bytes 1572868
  2.1 8.0 %collective-permute-start = (f32[17,32,128]{2,1,0:T(8,128)S(1)}, f32[17,32,128]{2,1,0:T(8,128)S(1)}, u32[]{:S(2)}, u32[]{:S(2)}) collective-permute-start(f32[17,32,128]{2,1,0:T(8,128)S(1)} %pad_maximum_fusion), channel_id=1, source_target_pairs={{0,32},{32,64},{64,96},{96,128},{128,160},{160,192},{192,224},{224... | collective-permute-start | bytes 835592 | tf_op jit(solution)/shard_map/ppermute | solution.py:490
  6.7 7.5 %collective-permute-start.1 = (f32[17,32,128]{2,1,0:T(8,128)S(1)}, f32[17,32,128]{2,1,0:T(8,128)S(1)}, u32[]{:S(2)}, u32[]{:S(2)}) collective-permute-start(f32[17,32,128]{2,1,0:T(8,128)S(1)} %pad_maximum_fusion.1), channel_id=1, source_target_pairs={{32,0},{64,32},{96,64},{128,96},{160,128},{192,160},{224,192},{256... | collective-permute-start | bytes 835592 | tf_op jit(solution)/shard_map/ppermute | solution.py:491
  14.2 15.3 %collective-permute-start.2 = (f32[624,128]{1,0:T(8,128)S(1)}, f32[624,128]{1,0:T(8,128)S(1)}, u32[]{:S(2)}, u32[]{:S(2)}) collective-permute-start(f32[624,128]{1,0:T(8,128)S(1)} %get-tuple-element.13), channel_id=1, source_target_pairs={{0,1},{1,2},{2,3},{3,4},{4,5},{5,6},{6,7},{7,8},{8,9},{9,10},{10,1... | collective-permute-start | bytes 958472 | tf_op jit(solution)/shard_map/ppermute | solution.py:495
  21.0 9.7 %collective-permute-start.3 = (f32[624,128]{1,0:T(8,128)S(1)}, f32[624,128]{1,0:T(8,128)S(1)}, u32[]{:S(2)}, u32[]{:S(2)}) collective-permute-start(f32[624,128]{1,0:T(8,128)S(1)} %get-tuple-element.14), channel_id=1, source_target_pairs={{1,0},{2,1},{3,2},{4,3},{5,4},{6,5},{7,6},{8,7},{9,8},{10,9},{11,1... | collective-permute-start | bytes 958472 | tf_op jit(solution)/shard_map/ppermute | solution.py:496

commit v3 on v2

--- a/solution.py
+++ b/solution.py
@@ -53,20 +53,47 @@
     return pltpu.with_memory_space_constraint(array, pltpu.VMEM)
 
 
+def in_hbm(array):
+    return pltpu.with_memory_space_constraint(array, pltpu.HBM)
+
+
 vmem = pl.BlockSpec(memory_space=pltpu.VMEM)
 leave = pl.BlockSpec(memory_space=pl.ANY)
 limits = pltpu.CompilerParams(vmem_limit_bytes=24 * 2**20)
 
 
-def strip_length(extent_x):
-    own = extent_x * len(own_rows())
-    return own, own + sum(rows for _, _, rows in corner_rows(extent_x))
+def pack_slabs(arrays):
+    extent_x = arrays[0].shape[0]
+    shape = (sum(WIDTHS), *arrays[0].shape[1:])
+
+    def kernel(*refs):
+        tails, heads, sems = refs[3:]
+        copies = []
+        for ref, width, at in zip(refs[:3], WIDTHS, (0, WIDTHS[0], WIDTHS[0] + WIDTHS[1])):
+            for start, target in ((extent_x - width, tails), (0, heads)):
+                source = ref.at[pl.ds(start, width)]
+                sem = sems.at[len(copies)]
+                copies.append(pltpu.make_async_copy(source, target.at[pl.ds(at, width)], sem))
+        for copy in copies:
+            copy.start()
+        for copy in copies:
+            copy.wait()
+
+    return pl.pallas_call(
+        kernel,
+        in_specs=[pl.BlockSpec(memory_space=pltpu.HBM)] * 3,
+        out_specs=[vmem] * 2,
+        out_shape=[vmem_result(shape)] * 2,
+        scratch_shapes=[pltpu.SemaphoreType.DMA((6,))],
+        compiler_params=limits,
+        name="pack_slabs",
+    )(*map(in_hbm, arrays))
 
 
 def pack_own(arrays):
     extent_x, extent_y = arrays[0].shape[:2]
     last = extent_y // TILE - 1
-    length = strip_length(extent_x)[0]
+    length = extent_x * len(own_rows())
 
     def kernel(*refs):
         low_refs, high_refs, up_ref, down_ref = refs[0:3], refs[3:6], refs[6], refs[7]
@@ -89,13 +116,11 @@
     )(*arrays, *arrays)
 
 
-def pack_corners(strips, slabs, extent_x):
-    own, length = strip_length(extent_x)
-
-    def kernel(own_up, own_down, low_ref, high_ref, up_ref, down_ref):
-        up_ref[0:own, :] = own_up[...]
-        down_ref[0:own, :] = own_down[...]
-        at = own
+def pack_corners(slabs, extent_x):
+    length = sum(rows for _, _, rows in corner_rows(extent_x))
+
+    def kernel(low_ref, high_ref, up_ref, down_ref):
+        at = 0
         for array, plane, rows in corner_rows(extent_x):
             side, where = slab_plane(array, plane, extent_x)
             slab = (low_ref, high_ref)[side]
@@ -106,12 +131,12 @@
 
     return pl.pallas_call(
         kernel,
-        in_specs=[vmem] * 4,
+        in_specs=[vmem] * 2,
         out_specs=[vmem] * 2,
         out_shape=[vmem_result((length, LANES))] * 2,
         compiler_params=limits,
         name="pack_corners",
-    )(*map(in_vmem, strips), *map(in_vmem, slabs))
+    )(*map(in_vmem, slabs))
 
 
 def plane_rolls(values, axis):
@@ -142,13 +167,13 @@
     return face_west
 
 
-def sweep(low, count, size, value_ref, source_ref, face_refs, term_ref, store):
+def sweep(low, count, size, value_ref, source_ref, face_refs, term_ref, store, rows=slice(None)):
     face_x, face_n, face_s, face_u, face_d, scales = face_refs
     limit = value_ref.shape[0] - 1
 
     def make_terms(planes, rolled):
         for plane, (up, down) in zip(planes, rolled):
-            term_ref[plane] = face_u[plane] * up + face_d[plane] * down
+            term_ref[plane, rows] = face_u[plane, rows] * up[rows] + face_d[plane, rows] * down[rows]
 
     def block(index, carried):
         before, value, face_west = carried
@@ -158,20 +183,21 @@
         for k in range(size):
             plane = base + k
             value_next = value_ref[plane + 1]
-            face_east = face_x[plane]
+            face_east = face_x[plane, rows]
             north, south = plane_rolls(value, 0)
-            near = (face_east * value_next + face_west * before) + (
-                face_n[plane] * north + face_s[plane] * south
+            near = (face_east * value_next[rows] + face_west * before) + (
+                face_n[plane, rows] * north[rows] + face_s[plane, rows] * south[rows]
             )
-            near = (near + term_ref[plane]) + source_ref[plane]
-            store(index, k, plane, (1.0 - relax_weight) * value + scales[plane] * near)
-            before, value, face_west = value, value_next, face_east
+            near = (near + term_ref[plane, rows]) + source_ref[plane, rows]
+            value_own = value[rows]
+            store(index, k, plane, (1.0 - relax_weight) * value_own + scales[plane, rows] * near)
+            before, value, face_west = value_own, value_next, face_east
         make_terms(ahead, rolled)
         return before, value, face_west
 
     planes = [low + k for k in range(size)]
     make_terms(planes, [plane_rolls(value_ref[plane], 1) for plane in planes])
-    start = (value_ref[low - 1], value_ref[low], face_x[low - 1])
+    start = (value_ref[low - 1, rows], value_ref[low], face_x[low - 1, rows])
     lax.fori_loop(0, count // size, block, start)
 
 
@@ -193,10 +219,9 @@
     return ext.at[pl.ds(REACH, extent_x), pl.ds(TILE, extent_y)]
 
 
-def place_halos(ext_refs, slab_refs, strip_refs, extent_x, extent_y, arrays):
+def place_halos(ext_refs, slab_refs, strip_refs, corner_refs, extent_x, extent_y):
     inner = slice(TILE, TILE + extent_y)
-    for array in arrays:
-        ext, width = ext_refs[array], WIDTHS[array]
+    for ext, width, start in zip(ext_refs, WIDTHS, (0, WIDTHS[0], WIDTHS[0] + WIDTHS[1])):
         planes = ext.shape[0]
         zeros = jnp.zeros((planes, TILE, LANES), jnp.float32)
         ext[:, 0:TILE, :] = zeros
@@ -204,30 +229,26 @@
         for plane in range(REACH - width):
             for side in (plane, planes - 1 - plane):
                 ext[side, inner, :] = jnp.zeros((extent_y, LANES), jnp.float32)
-        start = sum(WIDTHS[:array])
         part = slice(start, start + width)
         ext[REACH - width : REACH, inner, :] = slab_refs[0][part]
         ext[REACH + extent_x : REACH + extent_x + width, inner, :] = slab_refs[1][part]
-    low_ref, high_ref = strip_refs
     for k, (array, row) in enumerate(own_rows()):
-        if array in arrays:
-            ext, rows = ext_refs[array], slice(k * extent_x, (k + 1) * extent_x)
-            own = slice(REACH, REACH + extent_x)
-            ext[own, TILE - WIDTHS[array] + row, :] = low_ref[rows, :]
-            ext[own, TILE + extent_y + row, :] = high_ref[rows, :]
-    at = strip_length(extent_x)[0]
+        ext, rows = ext_refs[array], slice(k * extent_x, (k + 1) * extent_x)
+        own = slice(REACH, REACH + extent_x)
+        ext[own, TILE - WIDTHS[array] + row, :] = strip_refs[0][rows, :]
+        ext[own, TILE + extent_y + row, :] = strip_refs[1][rows, :]
+    at = 0
     for array, plane, rows in corner_rows(extent_x):
-        if array in arrays:
-            ext = ext_refs[array]
-            ext[plane, TILE - rows : TILE, :] = low_ref[at : at + rows, :]
-            ext[plane, TILE + extent_y : TILE + extent_y + rows, :] = high_ref[at : at + rows, :]
+        ext, part = ext_refs[array], slice(at, at + rows)
+        ext[plane, TILE - rows : TILE, :] = corner_refs[0][part, :]
+        ext[plane, TILE + extent_y : TILE + extent_y + rows, :] = corner_refs[1][part, :]
         at += rows
 
 
 def before_kernel(
-    cond_in, source_in, value_in, slab_low, slab_high, strip_low, strip_high, row_ref, value_out,
-    cond_ext, source_ext, value_ext, other, term, face_x, face_n, face_s, face_u, face_d, scales,
-    sems, out_sem,
+    cond_in, source_in, value_in, slab_low, slab_high, strip_low, strip_high, corner_low,
+    corner_high, row_ref, other, source_ext, face_x, face_n, face_s, face_u, face_d, scales,
+    cond_ext, value_ext, term, sems,
 ):
     extent_x, extent_y = cond_in.shape[0], cond_in.shape[1]
     planes = extent_x + 2 * REACH
@@ -239,7 +260,12 @@
     ]
     copies = start_copies(pairs, sems)
     place_halos(
-        exts, (slab_low, slab_high), (strip_low, strip_high), extent_x, extent_y, (0, 1, 2)
+        exts,
+        (slab_low, slab_high),
+        (strip_low, strip_high),
+        (corner_low, corner_high),
+        extent_x,
+        extent_y,
     )
     blank = jnp.zeros(cond_ext.shape[1:], jnp.float32)
     other[0] = blank
@@ -248,15 +274,13 @@
         copy.wait()
 
     def prepare_block(index, face_west):
-        return prepare(4 * index, 4, cond_ext, face_refs, face_west)
-
-    lax.fori_loop(0, planes // 4, prepare_block, blank)
+        return prepare(11 * index, 11, cond_ext, face_refs, face_west)
+
+    lax.fori_loop(0, planes // 11, prepare_block, blank)
     shared = (source_ext, face_refs, term)
-    sweep(1, planes - 2, 3, value_ext, *shared, keep_in(other))
-    sweep(1, planes - 2, 3, other, *shared, keep_in(value_ext))
-    sweep(1, planes - 2, 3, value_ext, *shared, keep_in(other))
-    kept = pltpu.make_async_copy(other.at[pl.ds(NU, planes - 2 * NU)], value_out, out_sem)
-    kept.start()
+    sweep(1, planes - 2, 14, value_ext, *shared, keep_in(other))
+    sweep(1, planes - 2, 14, other, *shared, keep_in(value_ext))
+    sweep(1, planes - 2, 14, value_ext, *shared, keep_in(other))
 
     inner = slice(TILE, TILE + extent_y)
     low_x, high_x = REACH, REACH + extent_x - 1
@@ -304,7 +328,6 @@
     row = jnp.where(place == 2 * SIDE, flow_east, row)
     row = jnp.where(place == SIDE, diag, row)
     row_ref[...] = jnp.where(place == 0, residual, row)
-    kept.wait()
 
 
 def total(values):
@@ -385,51 +408,21 @@
 
 def after_kernel(turn, counts):
     def kernel(
-        packed_ref, cond_in, source_in, value_in, slab_low, slab_high, strip_low, strip_high,
-        out_ref, cond_ext, source_ext, value_ext, other, term, face_x, face_n, face_s, face_u,
-        face_d, scales, out_part, sems, out_sems,
+        packed_ref, value_in, source_ext, face_x, face_n, face_s, face_u, face_d, scales, out_ref,
+        value_ext, other, term, out_part, out_sems,
     ):
-        extent_x, extent_y = cond_in.shape[0], cond_in.shape[1]
+        extent_x, extent_y = out_ref.shape[0], out_ref.shape[1]
         planes = extent_x + 2 * REACH
-        exts = (cond_ext, source_ext)
         face_refs = (face_x, face_n, face_s, face_u, face_d, scales)
-        copies = start_copies(
-            [
-                (cond_in, own_part(cond_ext, extent_x, extent_y)),
-                (source_in, own_part(source_ext, extent_x, extent_y)),
-                (value_in, value_ext.at[pl.ds(NU, planes - 2 * NU)]),
-            ],
-            sems,
-        )
-        place_halos(
-            exts, (slab_low, slab_high), (strip_low, strip_high), extent_x, extent_y, (0, 1)
-        )
+        low = NU + 1
         state, iterate_once = coarse_solver(packed_ref, turn, *counts)
-        low = NU + 1
-        pairs = (planes - 2 * low) // 2
-        lead = min(6, max(CG_ITERS - 1 - pairs, 0))
-        state = lax.fori_loop(0, lead, lambda i, s: iterate_once(s), state)
-        for copy in copies:
-            copy.wait()
-        face_west = 0.5 * (cond_ext[low - 1] + cond_ext[low])
-        face_x[low - 1] = face_west
-
-        def both(index, carried):
-            face_west = prepare(low + 2 * index, 2, cond_ext, face_refs, carried[1])
-            return iterate_once(carried[0]), face_west
-
-        shared = min(pairs, CG_ITERS - 1 - lead)
-        state, face_west = lax.fori_loop(0, shared, both, (state, face_west))
-        if shared < pairs:
-            prepare(low + 2 * shared, 2 * (pairs - shared), cond_ext, face_refs, face_west)
-        rest = CG_ITERS - 1 - lead - shared
-        state = lax.fori_loop(0, rest, lambda i, s: iterate_once(s), state)
+        state = lax.fori_loop(0, CG_ITERS - 1, lambda i, s: iterate_once(s), state)
         estimate = state[0]
 
         brick_x, brick_y = brick_index(estimate.shape)
         step_x = brick_x - lax.axis_index("gx")
         step_y = brick_y - lax.axis_index("gy")
-        row = lax.broadcasted_iota(jnp.int32, cond_ext.shape[1:], 0)
+        row = lax.broadcasted_iota(jnp.int32, value_in.shape[1:], 0)
 
         def lift_of(step):
             low, own, high = (
@@ -441,8 +434,8 @@
         lifts = [lift_of(step) for step in (-1, 0, 1)]
 
         def lift(plane, amount):
-            inside = cond_ext[plane] > 0
-            value_ext[plane] = value_ext[plane] + jnp.where(inside, amount, 0.0)
+            inside = scales[plane] > 0
+            value_ext[plane] = value_in[plane] + jnp.where(inside, amount, 0.0)
 
         for k in range(NU):
             lift(NU + k, lifts[0])
@@ -456,24 +449,40 @@
         lax.fori_loop(0, extent_x // 4, lift_block, 0)
 
         shared = (source_ext, face_refs, term)
-        sweep(low, planes - 2 * low, 3, value_ext, *shared, keep_in(other))
-        sweep(low + 1, planes - 2 * low, 3, other, *shared, keep_in(value_ext))
-        size = 4
+        sweep(low, planes - 2 * low, 12, value_ext, *shared, keep_in(other))
+        sweep(low + 1, planes - 2 * low, 12, other, *shared, keep_in(value_ext))
+        size = 8
 
         def part(index):
             rows = pl.ds(index * size, size)
             return pltpu.make_async_copy(out_part.at[rows], out_ref.at[rows], out_sems.at[index])
 
         def finish(index, k, plane, value):
-            out_part[index * size + k] = value[TILE : TILE + extent_y]
+            out_part[index * size + k] = value
             if k == size - 1:
                 part(index).start()
 
-        sweep(REACH, extent_x, size, value_ext, *shared, finish)
+        inner = slice(TILE, TILE + extent_y)
+        sweep(REACH, extent_x, size, value_ext, *shared, finish, inner)
         for index in range(extent_x // size):
             part(index).wait()
 
     return kernel
+
+
+def add_rows(gathered, count):
+    def kernel(rows_ref, out_ref):
+        row = jnp.sum(rows_ref[...], axis=0, keepdims=True)
+        out_ref[...] = jnp.broadcast_to(row, out_ref.shape)
+
+    return pl.pallas_call(
+        kernel,
+        in_specs=[vmem],
+        out_specs=vmem,
+        out_shape=vmem_result((count, LANES)),
+        compiler_params=pltpu.CompilerParams(vmem_limit_bytes=2**20),
+        name="add_rows",
+    )(in_vmem(gathered))
 
 
 def spread(rows, axis, order):
@@ -484,50 +493,50 @@
     arrays = (conductivity, source, initial)
     extent_x, extent_y = conductivity.shape[:2]
     count_x, count_y = lax.axis_size("gx"), lax.axis_size("gy")
-    tails = jnp.concatenate([a[extent_x - w :] for a, w in zip(arrays, WIDTHS)], 0)
-    heads = jnp.concatenate([a[:w] for a, w in zip(arrays, WIDTHS)], 0)
+    tails, heads = pack_slabs(arrays)
     slabs = (
         lax.ppermute(tails, "gx", ring_pairs(count_x, 1)),
         lax.ppermute(heads, "gx", ring_pairs(count_x, -1)),
     )
-    up, down = pack_corners(pack_own(arrays), slabs, extent_x)
-    strips = (
-        lax.ppermute(up, "gy", ring_pairs(count_y, 1)),
-        lax.ppermute(down, "gy", ring_pairs(count_y, -1)),
-    )
-    halos = [in_vmem(a) for a in (*slabs, *strips)]
-    planes, rows = extent_x + 2 * REACH, extent_y + 2 * TILE
-    scratch = [vmem_array((planes, rows, LANES))] * 11 + [pltpu.SemaphoreType.DMA((3,))]
-    row, smoothed = pl.pallas_call(
+
+    def along_y(pair):
+        up, down = pair
+        return (
+            lax.ppermute(up, "gy", ring_pairs(count_y, 1)),
+            lax.ppermute(down, "gy", ring_pairs(count_y, -1)),
+        )
+
+    strips = along_y(pack_own(arrays))
+    corners = along_y(pack_corners(slabs, extent_x))
+    halos = [in_vmem(a) for a in (*slabs, *strips, *corners)]
+    shape = (extent_x + 2 * REACH, extent_y + 2 * TILE, LANES)
+    row, *fields = pl.pallas_call(
         before_kernel,
-        in_specs=[leave] * 3 + [vmem] * 4,
-        out_specs=[vmem, leave],
-        out_shape=[
-            jax.ShapeDtypeStruct((count_y, LANES), jnp.float32),
-            jax.ShapeDtypeStruct((planes - 2 * NU, rows, LANES), jnp.float32),
-        ],
-        scratch_shapes=scratch + [pltpu.SemaphoreType.DMA],
+        in_specs=[leave] * 3 + [vmem] * 6,
+        out_specs=[vmem] * 9,
+        out_shape=[vmem_result((count_y, LANES))] + [vmem_result(shape)] * 8,
+        scratch_shapes=[vmem_array(shape)] * 3 + [pltpu.SemaphoreType.DMA((3,))],
         compiler_params=limits,
         name="smooth_before",
     )(*arrays, *halos)
-    row = jnp.sum(spread(row, "gy", list(range(count_y))), axis=0, keepdims=True)
+    rows = add_rows(spread(row, "gy", list(range(count_y))), count_x)
     half = count_x // 2
     order = list(range(half, count_x)) + list(range(half))
-    packed = spread(jnp.broadcast_to(row, (count_x, LANES)), "gx", order)
+    packed = spread(rows, "gx", order)
     turn = SIDE // TILE // 2
     if count_x != SIDE:
         packed = jnp.pad(jnp.roll(packed, half, 0), ((0, SIDE - count_x), (0, 0)))
         turn = 0
     return pl.pallas_call(
         after_kernel(turn, (count_x, count_y)),
-        in_specs=[vmem] + [leave] * 3 + [vmem] * 4,
+        in_specs=[vmem] * 9,
         out_specs=leave,
         out_shape=jax.ShapeDtypeStruct(conductivity.shape, jnp.float32),
-        scratch_shapes=scratch[:-1]
-        + [vmem_array(conductivity.shape), scratch[-1], pltpu.SemaphoreType.DMA((extent_x // 4,))],
+        scratch_shapes=[vmem_array(shape)] * 3
+        + [vmem_array(conductivity.shape), pltpu.SemaphoreType.DMA((extent_x // 8,))],
         compiler_params=limits,
         name="smooth_after",
-    )(packed, conductivity, source, smoothed, *halos)
+    )(*map(in_vmem, (packed, *fields)))
 
 
 def solution(mesh):

time: 98.6 us -> 91.1 us (0.924)
  waiting for transfers between devices: 6.97 us -> 0.83 us
  starting transfers between devices: 21 us -> 26.6 us
  Pallas kernels: 18.4 us -> 14.7 us
  local copies, waits for them, and re-layouts: 2.09 us -> 0.01 us
  blocking collectives: 49.4 us -> 48.3 us
    ppermute x2 -> x4, starting transfers between devices: 15.2 us -> 20.9 us  [the longest x2 15 us: along_y(): lax.ppermute(down, 'gy', ring_pairs(count_y, -1))]
    ppermute x1, waiting for transfers between devices: 4.03 us -> 0.01 us  [body(): lax.ppermute(heads, 'gx', ring_pairs(count_x, -1))]
    pallas_call x3 -> x5, Pallas kernels: 18.1 us -> 14.3 us  [the longest x1 7.26 us: body(): pl.pallas_call(after_kernel(turn, (count_x, count_y)), in_specs=[vmem] *...]
    slice x2 -> x0, local copies, waits for them, and re-layouts: 2.06 us -> none  [body(): heads = jnp.concatenate([a[:w] for a, w in zip(arrays, WIDTHS)], 0)]
    ppermute x1, waiting for transfers between devices: 1.73 us -> 0.01 us  [body(): lax.ppermute(tails, 'gx', ring_pairs(count_x, 1))]
    all_to_all x2, blocking collectives: 49.4 us -> 48.3 us  [spread(): lax.all_to_all(rows, axis, 0, 0, tiled=True, axis_index_groups=[order])]
  transfers between devices with their start and end apart: 4 -> 6, of which waited for: 3 -> 1; matrix products, arithmetic and copies ran while one was open for 0% -> 0% of each run, Pallas kernels for 0% -> 0%
where the time goes in v3:
time: 91.1 us; the launch traced here: 90.6 us
  blocking collectives  48.3 us (53%)
  starting transfers between devices  26.6 us (29%)
  Pallas kernels  14.7 us (16%)
    all_to_all x2, blocking collectives, spread(): lax.all_to_all(rows, axis, 0, 0, tiled=True, axis_index_groups=[order])  48.3 us
    ppermute x2, starting transfers between devices, along_y(): lax.ppermute(down, 'gy', ring_pairs(count_y, -1))  15 us
    pallas_call x1, Pallas kernels, body(): pl.pallas_call(after_kernel(turn, (count_x, count_y)), in_specs=[vmem] *...  7.26 us
    ppermute x2, starting transfers between devices, along_y(): lax.ppermute(up, 'gy', ring_pairs(count_y, 1))  5.97 us
    pallas_call x1, Pallas kernels, body(): pl.pallas_call(before_kernel, in_specs=[leave] * 3 + [vmem] * 6, out_spec...  5.75 us
    ppermute x1, starting transfers between devices, body(): lax.ppermute(tails, 'gx', ring_pairs(count_x, 1))  4.38 us
  transfers between devices with their start and end apart: 6, of which 1 were waited for; matrix products, arithmetic and copies ran while one was open for 0% of the time, Pallas kernels for 0%

profile of v3, /device:TPU:1, one launch (start us, length us, event | category | flops | bytes accessed | tf_op | source)
XLA Modules:
  0.0 90.6 jit_solution(4794914155181070782)
XLA Ops:
  0.0 0.0 copy-start.2
  0.0 0.0 copy-start.1
  0.0 0.0 copy-start
  0.0 1.3 %pack_slabs.1 = (f32[17,32,128]{2,1,0:T(8,128)S(1)}, f32[17,32,128]{2,1,0:T(8,128)S(1)}) custom-call(f32[32,32,128]{2,1,0:T(8,128)} %cond_in.1, f32[32,32,128]{2,1,0:T(8,128)} %source_in.1, f32[32,32,128]{2,1,0:T(8,128)} %value_in.1), custom_call_target="tpu_custom_call" | custom-call | tf_op jit(solution)/shard_map/pack_slabs/pallas_call | solution.py:82
  1.3 4.4 %collective-permute-start = (f32[17,32,128]{2,1,0:T(8,128)S(1)}, f32[17,32,128]{2,1,0:T(8,128)S(1)}, u32[]{:S(2)}, u32[]{:S(2)}) collective-permute-start(f32[17,32,128]{2,1,0:T(8,128)S(1)} %get-tuple-element.20), channel_id=1, source_target_pairs={{0,32},{32,64},{64,96},{96,128},{128,160},{160,192},{192,224},{224... | collective-permute-start | bytes 835592 | tf_op jit(solution)/shard_map/ppermute | solution.py:498
  5.7 1.3 %collective-permute-start.1 = (f32[17,32,128]{2,1,0:T(8,128)S(1)}, f32[17,32,128]{2,1,0:T(8,128)S(1)}, u32[]{:S(2)}, u32[]{:S(2)}) collective-permute-start(f32[17,32,128]{2,1,0:T(8,128)S(1)} %get-tuple-element.21), channel_id=1, source_target_pairs={{32,0},{64,32},{96,64},{128,96},{160,128},{192,160},{224,192},{256... | collective-permute-start | bytes 835592 | tf_op jit(solution)/shard_map/ppermute | solution.py:499
  7.0 0.0 copy-done.2
  7.0 0.0 copy-done.1
  7.0 0.0 copy-done
  7.0 0.4 pack_own.1
  7.4 4.0 %collective-permute-start.2 = (f32[544,128]{1,0:T(8,128)S(1)}, f32[544,128]{1,0:T(8,128)S(1)}, u32[]{:S(2)}, u32[]{:S(2)}) collective-permute-start(f32[544,128]{1,0:T(8,128)S(1)} %get-tuple-element.22), channel_id=1, source_target_pairs={{0,1},{1,2},{2,3},{3,4},{4,5},{5,6},{6,7},{7,8},{8,9},{9,10},{10,1... | collective-permute-start | bytes 835592 | tf_op jit(solution)/shard_map/ppermute | solution.py:505
  11.4 10.2 %collective-permute-start.3 = (f32[544,128]{1,0:T(8,128)S(1)}, f32[544,128]{1,0:T(8,128)S(1)}, u32[]{:S(2)}, u32[]{:S(2)}) collective-permute-start(f32[544,128]{1,0:T(8,128)S(1)} %get-tuple-element.23), channel_id=1, source_target_pairs={{1,0},{2,1},{3,2},{4,3},{5,4},{6,5},{7,6},{8,7},{9,8},{10,9},{11,1... | collective-permute-start | bytes 835592 | tf_op jit(solution)/shard_map/ppermute | solution.py:506
  21.7 0.0 collective-permute-done.low_ref.slab_low
  21.7 0.0 collective-permute-done.1.high_ref.slab_high
  21.7 1.9 %collective-permute-start.4 = (f32[80,128]{1,0:T(8,128)S(1)}, f32[80,128]{1,0:T(8,128)S(1)}, u32[]{:S(2)}, u32[]{:S(2)}) collective-permute-start(f32[80,128]{1,0:T(8,128)S(1)} %get-tuple-element.24), channel_id=1, source_target_pairs={{0,1},{1,2},{2,3},{3,4},{4,5},{5,6},{6,7},{7,8},{8,9},{9,10},{10,1... | collective-permute-start | bytes 122888 | tf_op jit(solution)/shard_map/ppermute | solution.py:505
  23.6 4.8 %collective-permute-start.5 = (f32[80,128]{1,0:T(8,128)S(1)}, f32[80,128]{1,0:T(8,128)S(1)}, u32[]{:S(2)}, u32[]{:S(2)}) collective-permute-start(f32[80,128]{1,0:T(8,128)S(1)} %get-tuple-element.25), channel_id=1, source_target_pairs={{1,0},{2,1},{3,2},{4,3},{5,4},{6,5},{7,6},{8,7},{9,8},{10,9},{11,1... | collective-permute-start | bytes 122888 | tf_op jit(solution)/shard_map/ppermute | solution.py:506
  28.4 0.0 collective-permute-done.2.strip_low
  28.4 0.0 collective-permute-done.3.strip_high
  28.4 0.0 collective-permute-done.4.corner_low
  28.4 0.8 collective-permute-done.5.corner_high
  29.3 5.8 %smooth_before.1 = (f32[32,128]{1,0:T(8,128)S(1)}, f32[44,48,128]{2,1,0:T(8,128)S(1)}, f32[44,48,128]{2,1,0:T(8,128)S(1)}, f32[44,48,128]{2,1,0:T(8,128)S(1)}, f...) custom-call(f32[32,32,128]{2,1,0:T(8,128)S(1)} %copy-done, ...), custom_call_target="tpu_custom_call" | custom-call | tf_op jit(solution)/shard_map/smooth_before/pallas_call | solution.py:513
  35.0 11.2 %all_to_all.22 = f32[32,1,128]{2,1,0:T(1,128)S(1)} all-to-all(f32[32,1,128]{2,1,0:T(1,128)S(1)} %bitcast.11), channel_id=1, replica_groups={{0,1,2,3,4,5,6,7,8,9,10,11,12,13,14,15,16,17,18,19,20,21,22,23,24,25,26..., dimensions={0} | all-to-all | bytes 32768 | tf_op jit(solution)/shard_map/all_to_all | solution.py:489
  46.2 37.1 %all_to_all.23 = f32[32,1,128]{2,1,0:T(1,128)S(1)} all-to-all(f32[32,1,128]{2,1,0:T(1,128)S(1)} %bitcast.10), channel_id=1, replica_groups={{512,544,576,608,640,672,704,736,768,800,832,864,896,928,960,992,0,32,6..., dimensions={0} | all-to-all | bytes 32768 | tf_op jit(solution)/shard_map/all_to_all | solution.py:489
  83.3 7.3 %smooth_after.1 = f32[32,32,128]{2,1,0:T(8,128)} custom-call(f32[32,128]{1,0:T(8,128)S(1)} %bitcast.8, f32[44,48,128]{2,1,0:T(8,128)S(1)} %get-tuple-element.27.value_in, f32[44,48,128]{2,1,0:T(8,128)S(1)} %get-tuple-element.28.source_ext, f32[44,48,128]{2,1,0:T(8,128)S(1)} %get-tuple-element.29.face_x, f32[44,48,128]{2,1,0:T(8,128)S(1)} %get-tuple-element.30.face_n, ...), custom_call_target="tpu_custom_call" | custom-call | tf_op jit(solution)/shard_map/smooth_after/pallas_call | solution.py:530
  (2 shorter events, 0.0 us)
Async XLA Ops:
  0.0 7.0 %copy-start.2 = (f32[32,32,128]{2,1,0:T(8,128)S(1)}, f32[32,32,128]{2,1,0:T(8,128)}, u32[]{:S(2)}) copy-start(f32[32,32,128]{2,1,0:T(8,128)} %value_in.1) | copy-start | bytes 1572868
  0.0 7.0 %copy-start.1 = (f32[32,32,128]{2,1,0:T(8,128)S(1)}, f32[32,32,128]{2,1,0:T(8,128)}, u32[]{:S(2)}) copy-start(f32[32,32,128]{2,1,0:T(8,128)} %source_in.1) | copy-start | bytes 1572868
  0.0 7.0 %copy-start = (f32[32,32,128]{2,1,0:T(8,128)S(1)}, f32[32,32,128]{2,1,0:T(8,128)}, u32[]{:S(2)}) copy-start(f32[32,32,128]{2,1,0:T(8,128)} %cond_in.1) | copy-start | bytes 1572868
  1.3 20.4 %collective-permute-start = (f32[17,32,128]{2,1,0:T(8,128)S(1)}, f32[17,32,128]{2,1,0:T(8,128)S(1)}, u32[]{:S(2)}, u32[]{:S(2)}) collective-permute-start(f32[17,32,128]{2,1,0:T(8,128)S(1)} %get-tuple-element.20), channel_id=1, source_target_pairs={{0,32},{32,64},{64,96},{96,128},{128,160},{160,192},{192,224},{224... | collective-permute-start | bytes 835592 | tf_op jit(solution)/shard_map/ppermute | solution.py:498
  5.7 16.0 %collective-permute-start.1 = (f32[17,32,128]{2,1,0:T(8,128)S(1)}, f32[17,32,128]{2,1,0:T(8,128)S(1)}, u32[]{:S(2)}, u32[]{:S(2)}) collective-permute-start(f32[17,32,128]{2,1,0:T(8,128)S(1)} %get-tuple-element.21), channel_id=1, source_target_pairs={{32,0},{64,32},{96,64},{128,96},{160,128},{192,160},{224,192},{256... | collective-permute-start | bytes 835592 | tf_op jit(solution)/shard_map/ppermute | solution.py:499
  7.4 21.0 %collective-permute-start.2 = (f32[544,128]{1,0:T(8,128)S(1)}, f32[544,128]{1,0:T(8,128)S(1)}, u32[]{:S(2)}, u32[]{:S(2)}) collective-permute-start(f32[544,128]{1,0:T(8,128)S(1)} %get-tuple-element.22), channel_id=1, source_target_pairs={{0,1},{1,2},{2,3},{3,4},{4,5},{5,6},{6,7},{7,8},{8,9},{9,10},{10,1... | collective-permute-start | bytes 835592 | tf_op jit(solution)/shard_map/ppermute | solution.py:505
  11.4 17.0 %collective-permute-start.3 = (f32[544,128]{1,0:T(8,128)S(1)}, f32[544,128]{1,0:T(8,128)S(1)}, u32[]{:S(2)}, u32[]{:S(2)}) collective-permute-start(f32[544,128]{1,0:T(8,128)S(1)} %get-tuple-element.23), channel_id=1, source_target_pairs={{1,0},{2,1},{3,2},{4,3},{5,4},{6,5},{7,6},{8,7},{9,8},{10,9},{11,1... | collective-permute-start | bytes 835592 | tf_op jit(solution)/shard_map/ppermute | solution.py:506
  21.7 6.7 %collective-permute-start.4 = (f32[80,128]{1,0:T(8,128)S(1)}, f32[80,128]{1,0:T(8,128)S(1)}, u32[]{:S(2)}, u32[]{:S(2)}) collective-permute-start(f32[80,128]{1,0:T(8,128)S(1)} %get-tuple-element.24), channel_id=1, source_target_pairs={{0,1},{1,2},{2,3},{3,4},{4,5},{5,6},{6,7},{7,8},{8,9},{9,10},{10,1... | collective-permute-start | bytes 122888 | tf_op jit(solution)/shard_map/ppermute | solution.py:505
  23.6 5.6 %collective-permute-start.5 = (f32[80,128]{1,0:T(8,128)S(1)}, f32[80,128]{1,0:T(8,128)S(1)}, u32[]{:S(2)}, u32[]{:S(2)}) collective-permute-start(f32[80,128]{1,0:T(8,128)S(1)} %get-tuple-element.25), channel_id=1, source_target_pairs={{1,0},{2,1},{3,2},{4,3},{5,4},{6,5},{7,6},{8,7},{9,8},{10,9},{11,1... | collective-permute-start | bytes 122888 | tf_op jit(solution)/shard_map/ppermute | solution.py:506

commit v4 on v3

--- a/solution.py
+++ b/solution.py
@@ -25,20 +25,12 @@
     return [(array, row) for array, width in enumerate(WIDTHS) for row in range(width)]
 
 
-def corner_rows(extent_x):
-    rows = []
-    for array, width in enumerate(WIDTHS):
-        for beyond in range(1, width):
-            for plane in (REACH - beyond, REACH + extent_x - 1 + beyond):
-                rows.append((array, plane, width - beyond))
-    return rows
-
-
-def slab_plane(array, plane, extent_x):
-    start = sum(WIDTHS[:array])
-    if plane < REACH:
-        return 0, start + plane - (REACH - WIDTHS[array])
-    return 1, start + plane - (REACH + extent_x)
+def corner_rows():
+    return [
+        (array, beyond, width - beyond)
+        for array, width in enumerate(WIDTHS)
+        for beyond in range(1, width)
+    ]
 
 
 def vmem_array(shape):
@@ -62,72 +54,60 @@
 limits = pltpu.CompilerParams(vmem_limit_bytes=24 * 2**20)
 
 
-def pack_slabs(arrays):
-    extent_x = arrays[0].shape[0]
-    shape = (sum(WIDTHS), *arrays[0].shape[1:])
+def pack_edges(arrays):
+    extent_x, extent_y = arrays[0].shape[:2]
+    starts = (0, WIDTHS[0], WIDTHS[0] + WIDTHS[1])
+    slab = (sum(WIDTHS), *arrays[0].shape[1:])
+    strip = (extent_x * len(own_rows()), LANES)
 
     def kernel(*refs):
-        tails, heads, sems = refs[3:]
-        copies = []
-        for ref, width, at in zip(refs[:3], WIDTHS, (0, WIDTHS[0], WIDTHS[0] + WIDTHS[1])):
-            for start, target in ((extent_x - width, tails), (0, heads)):
-                source = ref.at[pl.ds(start, width)]
-                sem = sems.at[len(copies)]
-                copies.append(pltpu.make_async_copy(source, target.at[pl.ds(at, width)], sem))
-        for copy in copies:
-            copy.start()
-        for copy in copies:
+        refs, (up, down, tails, heads), edges, sems = refs[:3], refs[3:7], refs[7:13], refs[13]
+        pairs = []
+        for k, ref in enumerate(refs):
+            pairs.append((ref.at[:, pl.ds(0, TILE)], edges[k]))
+            pairs.append((ref.at[:, pl.ds(extent_y - TILE, TILE)], edges[3 + k]))
+        for ref, width, at in zip(refs, WIDTHS, starts):
+            pairs.append((ref.at[pl.ds(extent_x - width, width)], tails.at[pl.ds(at, width)]))
+            pairs.append((ref.at[pl.ds(0, width)], heads.at[pl.ds(at, width)]))
+        copies = start_copies(pairs, sems)
+        for copy in copies[:6]:
             copy.wait()
-
-    return pl.pallas_call(
-        kernel,
-        in_specs=[pl.BlockSpec(memory_space=pltpu.HBM)] * 3,
-        out_specs=[vmem] * 2,
-        out_shape=[vmem_result(shape)] * 2,
-        scratch_shapes=[pltpu.SemaphoreType.DMA((6,))],
-        compiler_params=limits,
-        name="pack_slabs",
-    )(*map(in_hbm, arrays))
-
-
-def pack_own(arrays):
-    extent_x, extent_y = arrays[0].shape[:2]
-    last = extent_y // TILE - 1
-    length = extent_x * len(own_rows())
-
-    def kernel(*refs):
-        low_refs, high_refs, up_ref, down_ref = refs[0:3], refs[3:6], refs[6], refs[7]
         for k, (array, row) in enumerate(own_rows()):
             rows = slice(k * extent_x, (k + 1) * extent_x)
-            up_ref[rows, :] = high_refs[array][:, TILE - WIDTHS[array] + row, :]
-            down_ref[rows, :] = low_refs[array][:, row, :]
-
-    def edge(array, block):
-        return pl.BlockSpec((array.shape[0], TILE, LANES), lambda i: (0, block, 0))
-
-    return pl.pallas_call(
+            up[rows, :] = edges[3 + array][:, TILE - WIDTHS[array] + row, :]
+            down[rows, :] = edges[array][:, row, :]
+        for copy in copies[6:]:
+            copy.wait()
+
+    results = pl.pallas_call(
         kernel,
-        grid=(1,),
-        in_specs=[edge(a, 0) for a in arrays] + [edge(a, last) for a in arrays],
-        out_specs=[vmem] * 2,
-        out_shape=[vmem_result((length, LANES))] * 2,
+        in_specs=[leave] * 3,
+        out_specs=[vmem] * 4,
+        out_shape=[vmem_result(strip)] * 2 + [vmem_result(slab)] * 2,
+        scratch_shapes=[vmem_array((extent_x, TILE, LANES))] * 6
+        + [pltpu.SemaphoreType.DMA((12,))],
         compiler_params=limits,
-        name="pack_own",
-    )(*arrays, *arrays)
-
-
-def pack_corners(slabs, extent_x):
-    length = sum(rows for _, _, rows in corner_rows(extent_x))
+        name="pack_edges",
+    )(*map(in_hbm, arrays))
+    return results[:2], results[2:]
+
+
+def pack_corners(strips, extent_x):
+    length = 2 * sum(rows for _, _, rows in corner_rows())
 
     def kernel(low_ref, high_ref, up_ref, down_ref):
         at = 0
-        for array, plane, rows in corner_rows(extent_x):
-            side, where = slab_plane(array, plane, extent_x)
-            slab = (low_ref, high_ref)[side]
-            last = slab.shape[1]
-            up_ref[at : at + rows, :] = slab[where, last - rows : last, :]
-            down_ref[at : at + rows, :] = slab[where, 0:rows, :]
-            at += rows
+        for array, beyond, rows in corner_rows():
+            first = sum(WIDTHS[:array])
+            low = (first + WIDTHS[array] - rows) * extent_x
+            high = first * extent_x
+            for ref, start in ((low_ref, low), (high_ref, high)):
+                for k in range(rows):
+                    line = start + k * extent_x
+                    last = line + extent_x - beyond
+                    up_ref[at : at + 1, :] = ref[last : last + 1, :]
+                    down_ref[at : at + 1, :] = ref[line + beyond - 1 : line + beyond, :]
+                    at += 1
 
     return pl.pallas_call(
         kernel,
@@ -136,7 +116,7 @@
         out_shape=[vmem_result((length, LANES))] * 2,
         compiler_params=limits,
         name="pack_corners",
-    )(*map(in_vmem, slabs))
+    )(*map(in_vmem, strips))
 
 
 def plane_rolls(values, axis):
@@ -167,36 +147,29 @@
     return face_west
 
 
-def sweep(low, count, size, value_ref, source_ref, face_refs, term_ref, store, rows=slice(None)):
+def sweep(low, count, size, value_ref, source_ref, face_refs, store, rows=slice(None)):
     face_x, face_n, face_s, face_u, face_d, scales = face_refs
-    limit = value_ref.shape[0] - 1
-
-    def make_terms(planes, rolled):
-        for plane, (up, down) in zip(planes, rolled):
-            term_ref[plane, rows] = face_u[plane, rows] * up[rows] + face_d[plane, rows] * down[rows]
 
     def block(index, carried):
         before, value, face_west = carried
-        base = low + index * size
-        ahead = [jnp.minimum(base + size + k, limit) for k in range(size)]
-        rolled = [plane_rolls(value_ref[plane], 1) for plane in ahead]
         for k in range(size):
-            plane = base + k
+            plane = low + index * size + k
             value_next = value_ref[plane + 1]
             face_east = face_x[plane, rows]
             north, south = plane_rolls(value, 0)
+            up, down = plane_rolls(value[rows], 1)
             near = (face_east * value_next[rows] + face_west * before) + (
                 face_n[plane, rows] * north[rows] + face_s[plane, rows] * south[rows]
             )
-            near = (near + term_ref[plane, rows]) + source_ref[plane, rows]
+            near = near + (face_u[plane, rows] * up + face_d[plane, rows] * down)
             value_own = value[rows]
-            store(index, k, plane, (1.0 - relax_weight) * value_own + scales[plane, rows] * near)
+            result = (1.0 - relax_weight) * value_own + scales[plane, rows] * (
+                near + source_ref[plane, rows]
+            )
+            store(index, k, plane, result)
             before, value, face_west = value_own, value_next, face_east
-        make_terms(ahead, rolled)
         return before, value, face_west
 
-    planes = [low + k for k in range(size)]
-    make_terms(planes, [plane_rolls(value_ref[plane], 1) for plane in planes])
     start = (value_ref[low - 1, rows], value_ref[low], face_x[low - 1, rows])
     lax.fori_loop(0, count // size, block, start)
 
@@ -238,17 +211,19 @@
         ext[own, TILE - WIDTHS[array] + row, :] = strip_refs[0][rows, :]
         ext[own, TILE + extent_y + row, :] = strip_refs[1][rows, :]
     at = 0
-    for array, plane, rows in corner_rows(extent_x):
-        ext, part = ext_refs[array], slice(at, at + rows)
-        ext[plane, TILE - rows : TILE, :] = corner_refs[0][part, :]
-        ext[plane, TILE + extent_y : TILE + extent_y + rows, :] = corner_refs[1][part, :]
-        at += rows
+    for array, beyond, rows in corner_rows():
+        ext = ext_refs[array]
+        for plane, ref in zip((REACH - beyond, REACH + extent_x - 1 + beyond), corner_refs):
+            ext[plane, TILE - rows : TILE, :] = ref[at : at + rows, :]
+            edge = TILE + extent_y
+            ext[plane, edge : edge + rows, :] = ref[at + rows : at + 2 * rows, :]
+        at += 2 * rows
 
 
 def before_kernel(
     cond_in, source_in, value_in, slab_low, slab_high, strip_low, strip_high, corner_low,
     corner_high, row_ref, other, source_ext, face_x, face_n, face_s, face_u, face_d, scales,
-    cond_ext, value_ext, term, sems,
+    cond_ext, value_ext, sems,
 ):
     extent_x, extent_y = cond_in.shape[0], cond_in.shape[1]
     planes = extent_x + 2 * REACH
@@ -277,10 +252,10 @@
         return prepare(11 * index, 11, cond_ext, face_refs, face_west)
 
     lax.fori_loop(0, planes // 11, prepare_block, blank)
-    shared = (source_ext, face_refs, term)
-    sweep(1, planes - 2, 14, value_ext, *shared, keep_in(other))
-    sweep(1, planes - 2, 14, other, *shared, keep_in(value_ext))
-    sweep(1, planes - 2, 14, value_ext, *shared, keep_in(other))
+    shared = (source_ext, face_refs)
+    sweep(1, planes - 2, 21, value_ext, *shared, keep_in(other))
+    sweep(1, planes - 2, 21, other, *shared, keep_in(value_ext))
+    sweep(1, planes - 2, 21, value_ext, *shared, keep_in(other))
 
     inner = slice(TILE, TILE + extent_y)
     low_x, high_x = REACH, REACH + extent_x - 1
@@ -409,7 +384,7 @@
 def after_kernel(turn, counts):
     def kernel(
         packed_ref, value_in, source_ext, face_x, face_n, face_s, face_u, face_d, scales, out_ref,
-        value_ext, other, term, out_part, out_sems,
+        value_ext, other, out_part, out_sems,
     ):
         extent_x, extent_y = out_ref.shape[0], out_ref.shape[1]
         planes = extent_x + 2 * REACH
@@ -448,10 +423,10 @@
 
         lax.fori_loop(0, extent_x // 4, lift_block, 0)
 
-        shared = (source_ext, face_refs, term)
-        sweep(low, planes - 2 * low, 12, value_ext, *shared, keep_in(other))
-        sweep(low + 1, planes - 2 * low, 12, other, *shared, keep_in(value_ext))
-        size = 8
+        shared = (source_ext, face_refs)
+        sweep(low, planes - 2 * low, 18, value_ext, *shared, keep_in(other))
+        sweep(low + 1, planes - 2 * low, 18, other, *shared, keep_in(value_ext))
+        size = 16
 
         def part(index):
             rows = pl.ds(index * size, size)
@@ -493,21 +468,17 @@
     arrays = (conductivity, source, initial)
     extent_x, extent_y = conductivity.shape[:2]
     count_x, count_y = lax.axis_size("gx"), lax.axis_size("gy")
-    tails, heads = pack_slabs(arrays)
-    slabs = (
-        lax.ppermute(tails, "gx", ring_pairs(count_x, 1)),
-        lax.ppermute(heads, "gx", ring_pairs(count_x, -1)),
-    )
-
-    def along_y(pair):
+    def along(axis, count, pair):
         up, down = pair
         return (
-            lax.ppermute(up, "gy", ring_pairs(count_y, 1)),
-            lax.ppermute(down, "gy", ring_pairs(count_y, -1)),
+            lax.ppermute(up, axis, ring_pairs(count, 1)),
+            lax.ppermute(down, axis, ring_pairs(count, -1)),
         )
 
-    strips = along_y(pack_own(arrays))
-    corners = along_y(pack_corners(slabs, extent_x))
+    strips, slabs = pack_edges(arrays)
+    strips = along("gy", count_y, strips)
+    slabs = along("gx", count_x, slabs)
+    corners = along("gx", count_x, pack_corners(strips, extent_x))
     halos = [in_vmem(a) for a in (*slabs, *strips, *corners)]
     shape = (extent_x + 2 * REACH, extent_y + 2 * TILE, LANES)
     row, *fields = pl.pallas_call(
@@ -515,11 +486,13 @@
         in_specs=[leave] * 3 + [vmem] * 6,
         out_specs=[vmem] * 9,
         out_shape=[vmem_result((count_y, LANES))] + [vmem_result(shape)] * 8,
-        scratch_shapes=[vmem_array(shape)] * 3 + [pltpu.SemaphoreType.DMA((3,))],
+        scratch_shapes=[vmem_array(shape)] * 2 + [pltpu.SemaphoreType.DMA((3,))],
         compiler_params=limits,
         name="smooth_before",
     )(*arrays, *halos)
-    rows = add_rows(spread(row, "gy", list(range(count_y))), count_x)
+    start = count_y // 3 + 1
+    order = [start, *(y for y in range(count_y) if y != start)]
+    rows = add_rows(spread(row, "gy", order), count_x)
     half = count_x // 2
     order = list(range(half, count_x)) + list(range(half))
     packed = spread(rows, "gx", order)
@@ -532,8 +505,8 @@
         in_specs=[vmem] * 9,
         out_specs=leave,
         out_shape=jax.ShapeDtypeStruct(conductivity.shape, jnp.float32),
-        scratch_shapes=[vmem_array(shape)] * 3
-        + [vmem_array(conductivity.shape), pltpu.SemaphoreType.DMA((extent_x // 8,))],
+        scratch_shapes=[vmem_array(shape)] * 2
+        + [vmem_array(conductivity.shape), pltpu.SemaphoreType.DMA((extent_x // 16,))],
         compiler_params=limits,
         name="smooth_after",
     )(*map(in_vmem, (packed, *fields)))

time: 91.1 us -> 85.3 us (0.936)
  blocking collectives: 48.3 us -> 43.1 us
  waiting for transfers between devices: 0.83 us -> 4.58 us
  Pallas kernels: 14.7 us -> 11.7 us
  starting transfers between devices: 26.6 us -> 25.2 us
    all_to_all x2, blocking collectives: 48.3 us -> 43.1 us  [spread(): lax.all_to_all(rows, axis, 0, 0, tiled=True, axis_index_groups=[order])]
    ppermute x6, waiting for transfers between devices: 0.83 us -> 4.58 us  [the longest x3 4.57 us: along(): lax.ppermute(down, axis, ring_pairs(count, -1))]
    pallas_call x1, Pallas kernels: 5.75 us -> 4.02 us  [body(): pl.pallas_call(before_kernel, in_specs=[leave] * 3 + [vmem] * 6, out_spec...]
    ppermute x6, starting transfers between devices: 26.6 us -> 25.2 us  [the longest x3 15.3 us: along(): lax.ppermute(down, axis, ring_pairs(count, -1))]
    pallas_call x1, Pallas kernels: 7.26 us -> 5.87 us  [body(): pl.pallas_call(after_kernel(turn, (count_x, count_y)), in_specs=[vmem] *...]
  transfers between devices with their start and end apart: 6 -> 6, of which waited for: 1 -> 2; matrix products, arithmetic and copies ran while one was open for 0% -> 0% of each run, Pallas kernels for 0% -> 0%
where the time goes in v4:
time: 85.3 us; the launch traced here: 84.7 us
  blocking collectives  43.1 us (51%)
  starting transfers between devices  25.2 us (30%)
  Pallas kernels  11.7 us (14%)
  waiting for transfers between devices  4.58 us (5%)
    all_to_all x2, blocking collectives, spread(): lax.all_to_all(rows, axis, 0, 0, tiled=True, axis_index_groups=[order])  43.1 us
    ppermute x3, starting transfers between devices, along(): lax.ppermute(down, axis, ring_pairs(count, -1))  15.3 us
    ppermute x3, starting transfers between devices, along(): lax.ppermute(up, axis, ring_pairs(count, 1))  9.88 us
    pallas_call x1, Pallas kernels, body(): pl.pallas_call(after_kernel(turn, (count_x, count_y)), in_specs=[vmem] *...  5.87 us
    ppermute x3, waiting for transfers between devices, along(): lax.ppermute(down, axis, ring_pairs(count, -1))  4.57 us
    pallas_call x1, Pallas kernels, body(): pl.pallas_call(before_kernel, in_specs=[leave] * 3 + [vmem] * 6, out_spec...  4.02 us
    pallas_call x1, Pallas kernels, pack_edges(): pl.pallas_call(kernel, in_specs=[leave] * 3, out_specs=[vmem] * 4, out_sh...  1.73 us
  transfers between devices with their start and end apart: 6, of which 2 were waited for; matrix products, arithmetic and copies ran while one was open for 0% of the time, Pallas kernels for 0%

profile of v4, /device:TPU:1, one launch (start us, length us, event | category | flops | bytes accessed | tf_op | source)
XLA Modules:
  0.0 84.7 jit_solution(206742961803238971)
XLA Ops:
  0.0 0.0 copy-start.2
  0.0 0.0 copy-start.1
  0.0 0.0 copy-start
  0.0 1.7 %pack_edges.1 = (f32[544,128]{1,0:T(8,128)S(1)}, f32[544,128]{1,0:T(8,128)S(1)}, f32[17,32,128]{2,1,0:T(8,128)S(1)}, f32[17,32,128]{2,1,0:T(8,128)S(1)}) custom-call(f32[32,32,128]{2,1,0:T(8,128)} %cond_in.1, f32[32,32,128]{2,1,0:T(8,128)} %source_in.1, f32[32,32,128]{2,1,0:T(8,128)} %value_in.1), custom_call_target="tpu_custom_call" | custom-call | tf_op jit(solution)/shard_map/pack_edges/pallas_call | solution.py:82
  1.7 4.6 %collective-permute-start.2 = (f32[544,128]{1,0:T(8,128)S(1)}, f32[544,128]{1,0:T(8,128)S(1)}, u32[]{:S(2)}, u32[]{:S(2)}) collective-permute-start(f32[544,128]{1,0:T(8,128)S(1)} %get-tuple-element.22), channel_id=1, source_target_pairs={{0,1},{1,2},{2,3},{3,4},{4,5},{5,6},{6,7},{7,8},{8,9},{9,10},{10,1... | collective-permute-start | bytes 835592 | tf_op jit(solution)/shard_map/ppermute | solution.py:474
  6.3 12.7 %collective-permute-start.3 = (f32[544,128]{1,0:T(8,128)S(1)}, f32[544,128]{1,0:T(8,128)S(1)}, u32[]{:S(2)}, u32[]{:S(2)}) collective-permute-start(f32[544,128]{1,0:T(8,128)S(1)} %get-tuple-element.23), channel_id=1, source_target_pairs={{1,0},{2,1},{3,2},{4,3},{5,4},{6,5},{7,6},{8,7},{9,8},{10,9},{11,1... | collective-permute-start | bytes 835592 | tf_op jit(solution)/shard_map/ppermute | solution.py:475
  19.1 1.3 %collective-permute-start = (f32[17,32,128]{2,1,0:T(8,128)S(1)}, f32[17,32,128]{2,1,0:T(8,128)S(1)}, u32[]{:S(2)}, u32[]{:S(2)}) collective-permute-start(f32[17,32,128]{2,1,0:T(8,128)S(1)} %get-tuple-element.20), channel_id=1, source_target_pairs={{0,32},{32,64},{64,96},{96,128},{128,160},{160,192},{192,224},{224... | collective-permute-start | bytes 835592 | tf_op jit(solution)/shard_map/ppermute | solution.py:474
  20.4 1.3 %collective-permute-start.1 = (f32[17,32,128]{2,1,0:T(8,128)S(1)}, f32[17,32,128]{2,1,0:T(8,128)S(1)}, u32[]{:S(2)}, u32[]{:S(2)}) collective-permute-start(f32[17,32,128]{2,1,0:T(8,128)S(1)} %get-tuple-element.21), channel_id=1, source_target_pairs={{32,0},{64,32},{96,64},{128,96},{160,128},{192,160},{224,192},{256... | collective-permute-start | bytes 835592 | tf_op jit(solution)/shard_map/ppermute | solution.py:475
  21.7 0.0 collective-permute-done.2.low_ref.strip_low
  21.7 0.0 collective-permute-done.3.high_ref.strip_high
  21.7 0.1 pack_corners.1
  21.8 4.0 %collective-permute-start.4 = (f32[80,128]{1,0:T(8,128)S(1)}, f32[80,128]{1,0:T(8,128)S(1)}, u32[]{:S(2)}, u32[]{:S(2)}) collective-permute-start(f32[80,128]{1,0:T(8,128)S(1)} %get-tuple-element.24), channel_id=1, source_target_pairs={{0,32},{32,64},{64,96},{96,128},{128,160},{160,192},{192,224},{224... | collective-permute-start | bytes 122888 | tf_op jit(solution)/shard_map/ppermute | solution.py:474
  25.8 1.3 %collective-permute-start.5 = (f32[80,128]{1,0:T(8,128)S(1)}, f32[80,128]{1,0:T(8,128)S(1)}, u32[]{:S(2)}, u32[]{:S(2)}) collective-permute-start(f32[80,128]{1,0:T(8,128)S(1)} %get-tuple-element.25), channel_id=1, source_target_pairs={{32,0},{64,32},{96,64},{128,96},{160,128},{192,160},{224,192},{256... | collective-permute-start | bytes 122888 | tf_op jit(solution)/shard_map/ppermute | solution.py:475
  27.1 0.0 collective-permute-done.slab_low
  27.1 3.7 %collective-permute-done.1.slab_high = f32[17,32,128]{2,1,0:T(8,128)S(1)} collective-permute-done((f32[17,32,128]{2,1,0:T(8,128)S(1)}, f32[17,32,128]{2,1,0:T(8,128)S(1)}, u32[]{:S(2)}, u32[]{:S(2)}) %collective-permute-start.1) | collective-permute-done | bytes 278560 | tf_op jit(solution)/shard_map/ppermute | solution.py:475
  30.8 0.0 collective-permute-done.4.corner_low
  30.8 0.8 collective-permute-done.5.corner_high
  31.7 0.0 copy-done.2
  31.7 0.0 copy-done.1
  31.7 0.0 copy-done
  31.7 4.0 %smooth_before.1 = (f32[32,128]{1,0:T(8,128)S(1)}, f32[44,48,128]{2,1,0:T(8,128)S(1)}, f32[44,48,128]{2,1,0:T(8,128)S(1)}, f32[44,48,128]{2,1,0:T(8,128)S(1)}, f...) custom-call(f32[32,32,128]{2,1,0:T(8,128)S(1)} %copy-done, ...), custom_call_target="tpu_custom_call" | custom-call | tf_op jit(solution)/shard_map/smooth_before/pallas_call | solution.py:484
  35.7 10.1 %all_to_all.22 = f32[32,1,128]{2,1,0:T(1,128)S(1)} all-to-all(f32[32,1,128]{2,1,0:T(1,128)S(1)} %bitcast.11), channel_id=1, replica_groups={{11,0,1,2,3,4,5,6,7,8,9,10,12,13,14,15,16,17,18,19,20,21,22,23,24,25,26..., dimensions={0} | all-to-all | bytes 32768 | tf_op jit(solution)/shard_map/all_to_all | solution.py:464
  45.8 33.0 %all_to_all.23 = f32[32,1,128]{2,1,0:T(1,128)S(1)} all-to-all(f32[32,1,128]{2,1,0:T(1,128)S(1)} %bitcast.10), channel_id=1, replica_groups={{512,544,576,608,640,672,704,736,768,800,832,864,896,928,960,992,0,32,6..., dimensions={0} | all-to-all | bytes 32768 | tf_op jit(solution)/shard_map/all_to_all | solution.py:464
  78.8 5.9 %smooth_after.1 = f32[32,32,128]{2,1,0:T(8,128)} custom-call(f32[32,128]{1,0:T(8,128)S(1)} %bitcast.8, f32[44,48,128]{2,1,0:T(8,128)S(1)} %get-tuple-element.27.value_in, f32[44,48,128]{2,1,0:T(8,128)S(1)} %get-tuple-element.28.source_ext, f32[44,48,128]{2,1,0:T(8,128)S(1)} %get-tuple-element.29.face_x, f32[44,48,128]{2,1,0:T(8,128)S(1)} %get-tuple-element.30.face_n, ...), custom_call_target="tpu_custom_call" | custom-call | tf_op jit(solution)/shard_map/smooth_after/pallas_call | solution.py:503
  (1 shorter events, 0.0 us)
Async XLA Ops:
  0.0 31.7 %copy-start.2 = (f32[32,32,128]{2,1,0:T(8,128)S(1)}, f32[32,32,128]{2,1,0:T(8,128)}, u32[]{:S(2)}) copy-start(f32[32,32,128]{2,1,0:T(8,128)} %value_in.1) | copy-start | bytes 1572868
  0.0 31.7 %copy-start.1 = (f32[32,32,128]{2,1,0:T(8,128)S(1)}, f32[32,32,128]{2,1,0:T(8,128)}, u32[]{:S(2)}) copy-start(f32[32,32,128]{2,1,0:T(8,128)} %source_in.1) | copy-start | bytes 1572868
  0.0 31.7 %copy-start = (f32[32,32,128]{2,1,0:T(8,128)S(1)}, f32[32,32,128]{2,1,0:T(8,128)}, u32[]{:S(2)}) copy-start(f32[32,32,128]{2,1,0:T(8,128)} %cond_in.1) | copy-start | bytes 1572868
  1.7 20.0 %collective-permute-start.2 = (f32[544,128]{1,0:T(8,128)S(1)}, f32[544,128]{1,0:T(8,128)S(1)}, u32[]{:S(2)}, u32[]{:S(2)}) collective-permute-start(f32[544,128]{1,0:T(8,128)S(1)} %get-tuple-element.22), channel_id=1, source_target_pairs={{0,1},{1,2},{2,3},{3,4},{4,5},{5,6},{6,7},{7,8},{8,9},{9,10},{10,1... | collective-permute-start | bytes 835592 | tf_op jit(solution)/shard_map/ppermute | solution.py:474
  6.3 15.4 %collective-permute-start.3 = (f32[544,128]{1,0:T(8,128)S(1)}, f32[544,128]{1,0:T(8,128)S(1)}, u32[]{:S(2)}, u32[]{:S(2)}) collective-permute-start(f32[544,128]{1,0:T(8,128)S(1)} %get-tuple-element.23), channel_id=1, source_target_pairs={{1,0},{2,1},{3,2},{4,3},{5,4},{6,5},{7,6},{8,7},{9,8},{10,9},{11,1... | collective-permute-start | bytes 835592 | tf_op jit(solution)/shard_map/ppermute | solution.py:475
  19.1 8.0 %collective-permute-start = (f32[17,32,128]{2,1,0:T(8,128)S(1)}, f32[17,32,128]{2,1,0:T(8,128)S(1)}, u32[]{:S(2)}, u32[]{:S(2)}) collective-permute-start(f32[17,32,128]{2,1,0:T(8,128)S(1)} %get-tuple-element.20), channel_id=1, source_target_pairs={{0,32},{32,64},{64,96},{96,128},{128,160},{160,192},{192,224},{224... | collective-permute-start | bytes 835592 | tf_op jit(solution)/shard_map/ppermute | solution.py:474
  20.4 10.4 %collective-permute-start.1 = (f32[17,32,128]{2,1,0:T(8,128)S(1)}, f32[17,32,128]{2,1,0:T(8,128)S(1)}, u32[]{:S(2)}, u32[]{:S(2)}) collective-permute-start(f32[17,32,128]{2,1,0:T(8,128)S(1)} %get-tuple-element.21), channel_id=1, source_target_pairs={{32,0},{64,32},{96,64},{128,96},{160,128},{192,160},{224,192},{256... | collective-permute-start | bytes 835592 | tf_op jit(solution)/shard_map/ppermute | solution.py:475
  21.8 9.1 %collective-permute-start.4 = (f32[80,128]{1,0:T(8,128)S(1)}, f32[80,128]{1,0:T(8,128)S(1)}, u32[]{:S(2)}, u32[]{:S(2)}) collective-permute-start(f32[80,128]{1,0:T(8,128)S(1)} %get-tuple-element.24), channel_id=1, source_target_pairs={{0,32},{32,64},{64,96},{96,128},{128,160},{160,192},{192,224},{224... | collective-permute-start | bytes 122888 | tf_op jit(solution)/shard_map/ppermute | solution.py:474
  25.8 5.9 %collective-permute-start.5 = (f32[80,128]{1,0:T(8,128)S(1)}, f32[80,128]{1,0:T(8,128)S(1)}, u32[]{:S(2)}, u32[]{:S(2)}) collective-permute-start(f32[80,128]{1,0:T(8,128)S(1)} %get-tuple-element.25), channel_id=1, source_target_pairs={{32,0},{64,32},{96,64},{128,96},{160,128},{192,160},{224,192},{256... | collective-permute-start | bytes 122888 | tf_op jit(solution)/shard_map/ppermute | solution.py:475

commit v5 on v4

--- a/solution.py
+++ b/solution.py
@@ -21,8 +21,13 @@
     return [(i, i + step) for i in range(count) if 0 <= i + step < count]
 
 
-def own_rows():
-    return [(array, row) for array, width in enumerate(WIDTHS) for row in range(width)]
+def own_rows(extent_x):
+    rows, at = [], 0
+    for array, width in enumerate(WIDTHS):
+        for plane in range(extent_x):
+            rows.append((array, plane, at))
+            at += width
+    return rows
 
 
 def corner_rows():
@@ -58,7 +63,7 @@
     extent_x, extent_y = arrays[0].shape[:2]
     starts = (0, WIDTHS[0], WIDTHS[0] + WIDTHS[1])
     slab = (sum(WIDTHS), *arrays[0].shape[1:])
-    strip = (extent_x * len(own_rows()), LANES)
+    strip = (extent_x * sum(WIDTHS), LANES)
 
     def kernel(*refs):
         refs, (up, down, tails, heads), edges, sems = refs[:3], refs[3:7], refs[7:13], refs[13]
@@ -72,10 +77,10 @@
         copies = start_copies(pairs, sems)
         for copy in copies[:6]:
             copy.wait()
-        for k, (array, row) in enumerate(own_rows()):
-            rows = slice(k * extent_x, (k + 1) * extent_x)
-            up[rows, :] = edges[3 + array][:, TILE - WIDTHS[array] + row, :]
-            down[rows, :] = edges[array][:, row, :]
+        for array, plane, at in own_rows(extent_x):
+            width = WIDTHS[array]
+            up[at : at + width, :] = edges[3 + array][plane, TILE - width : TILE, :]
+            down[at : at + width, :] = edges[array][plane, 0:width, :]
         for copy in copies[6:]:
             copy.wait()
 
@@ -98,16 +103,13 @@
     def kernel(low_ref, high_ref, up_ref, down_ref):
         at = 0
         for array, beyond, rows in corner_rows():
-            first = sum(WIDTHS[:array])
-            low = (first + WIDTHS[array] - rows) * extent_x
-            high = first * extent_x
-            for ref, start in ((low_ref, low), (high_ref, high)):
-                for k in range(rows):
-                    line = start + k * extent_x
-                    last = line + extent_x - beyond
-                    up_ref[at : at + 1, :] = ref[last : last + 1, :]
-                    down_ref[at : at + 1, :] = ref[line + beyond - 1 : line + beyond, :]
-                    at += 1
+            width = WIDTHS[array]
+            first = sum(WIDTHS[:array]) * extent_x
+            for out, plane in ((up_ref, extent_x - beyond), (down_ref, beyond - 1)):
+                start = first + plane * width
+                out[at : at + rows, :] = low_ref[start + width - rows : start + width, :]
+                out[at + rows : at + 2 * rows, :] = high_ref[start : start + rows, :]
+            at += 2 * rows
 
     return pl.pallas_call(
         kernel,
@@ -205,17 +207,16 @@
         part = slice(start, start + width)
         ext[REACH - width : REACH, inner, :] = slab_refs[0][part]
         ext[REACH + extent_x : REACH + extent_x + width, inner, :] = slab_refs[1][part]
-    for k, (array, row) in enumerate(own_rows()):
-        ext, rows = ext_refs[array], slice(k * extent_x, (k + 1) * extent_x)
-        own = slice(REACH, REACH + extent_x)
-        ext[own, TILE - WIDTHS[array] + row, :] = strip_refs[0][rows, :]
-        ext[own, TILE + extent_y + row, :] = strip_refs[1][rows, :]
+    edge = TILE + extent_y
+    for array, plane, at in own_rows(extent_x):
+        ext, width = ext_refs[array], WIDTHS[array]
+        ext[REACH + plane, TILE - width : TILE, :] = strip_refs[0][at : at + width, :]
+        ext[REACH + plane, edge : edge + width, :] = strip_refs[1][at : at + width, :]
     at = 0
     for array, beyond, rows in corner_rows():
         ext = ext_refs[array]
         for plane, ref in zip((REACH - beyond, REACH + extent_x - 1 + beyond), corner_refs):
             ext[plane, TILE - rows : TILE, :] = ref[at : at + rows, :]
-            edge = TILE + extent_y
             ext[plane, edge : edge + rows, :] = ref[at + rows : at + 2 * rows, :]
         at += 2 * rows
 
@@ -243,8 +244,6 @@
         extent_y,
     )
     blank = jnp.zeros(cond_ext.shape[1:], jnp.float32)
-    other[0] = blank
-    other[planes - 1] = blank
     for copy in copies:
         copy.wait()
 
@@ -253,9 +252,9 @@
 
     lax.fori_loop(0, planes // 11, prepare_block, blank)
     shared = (source_ext, face_refs)
-    sweep(1, planes - 2, 21, value_ext, *shared, keep_in(other))
-    sweep(1, planes - 2, 21, other, *shared, keep_in(value_ext))
-    sweep(1, planes - 2, 21, value_ext, *shared, keep_in(other))
+    sweep(1, planes - 2, planes // 2 - 1, value_ext, *shared, keep_in(other))
+    sweep(2, planes - 4, planes // 2 - 2, other, *shared, keep_in(value_ext))
+    sweep(3, planes - 6, planes // 2 - 3, value_ext, *shared, keep_in(other))
 
     inner = slice(TILE, TILE + extent_y)
     low_x, high_x = REACH, REACH + extent_x - 1
@@ -424,8 +423,9 @@
         lax.fori_loop(0, extent_x // 4, lift_block, 0)
 
         shared = (source_ext, face_refs)
-        sweep(low, planes - 2 * low, 18, value_ext, *shared, keep_in(other))
-        sweep(low + 1, planes - 2 * low, 18, other, *shared, keep_in(value_ext))
+        half = planes // 2 - low
+        sweep(low, 2 * half, half, value_ext, *shared, keep_in(other))
+        sweep(low + 1, 2 * half - 2, half - 1, other, *shared, keep_in(value_ext))
         size = 16
 
         def part(index):

time: 85.3 us -> 84.7 us (level)
  no operation moved by 1% of the time
where the time goes in v5:
time: 84.7 us; the launch traced here: 84.1 us
  blocking collectives  43.1 us (51%)
  starting transfers between devices  25.2 us (30%)
  Pallas kernels  11.1 us (13%)
  waiting for transfers between devices  4.58 us (5%)
    all_to_all x2, blocking collectives, spread(): lax.all_to_all(rows, axis, 0, 0, tiled=True, axis_index_groups=[order])  43.1 us
    ppermute x3, starting transfers between devices, along(): lax.ppermute(down, axis, ring_pairs(count, -1))  15.3 us
    ppermute x3, starting transfers between devices, along(): lax.ppermute(up, axis, ring_pairs(count, 1))  9.88 us
    pallas_call x1, Pallas kernels, body(): pl.pallas_call(after_kernel(turn, (count_x, count_y)), in_specs=[vmem] *...  5.87 us
    ppermute x3, waiting for transfers between devices, along(): lax.ppermute(down, axis, ring_pairs(count, -1))  4.57 us
    pallas_call x1, Pallas kernels, body(): pl.pallas_call(before_kernel, in_specs=[leave] * 3 + [vmem] * 6, out_spec...  3.64 us
  transfers between devices with their start and end apart: 6, of which 2 were waited for; matrix products, arithmetic and copies ran while one was open for 0% of the time, Pallas kernels for 0%

profile of v5, /device:TPU:1, one launch (start us, length us, event | category | flops | bytes accessed | tf_op | source)
XLA Modules:
  0.0 84.1 jit_solution(13276645552336115211)
XLA Ops:
  0.0 0.0 copy-start.2
  0.0 0.0 copy-start.1
  0.0 0.0 copy-start
  0.0 1.6 %pack_edges.1 = (f32[544,128]{1,0:T(8,128)S(1)}, f32[544,128]{1,0:T(8,128)S(1)}, f32[17,32,128]{2,1,0:T(8,128)S(1)}, f32[17,32,128]{2,1,0:T(8,128)S(1)}) custom-call(f32[32,32,128]{2,1,0:T(8,128)} %cond_in.1, f32[32,32,128]{2,1,0:T(8,128)} %source_in.1, f32[32,32,128]{2,1,0:T(8,128)} %value_in.1), custom_call_target="tpu_custom_call" | custom-call | tf_op jit(solution)/shard_map/pack_edges/pallas_call | solution.py:87
  1.6 4.6 %collective-permute-start.2 = (f32[544,128]{1,0:T(8,128)S(1)}, f32[544,128]{1,0:T(8,128)S(1)}, u32[]{:S(2)}, u32[]{:S(2)}) collective-permute-start(f32[544,128]{1,0:T(8,128)S(1)} %get-tuple-element.22), channel_id=1, source_target_pairs={{0,1},{1,2},{2,3},{3,4},{4,5},{5,6},{6,7},{7,8},{8,9},{9,10},{10,1... | collective-permute-start | bytes 835592 | tf_op jit(solution)/shard_map/ppermute | solution.py:474
  6.2 12.7 %collective-permute-start.3 = (f32[544,128]{1,0:T(8,128)S(1)}, f32[544,128]{1,0:T(8,128)S(1)}, u32[]{:S(2)}, u32[]{:S(2)}) collective-permute-start(f32[544,128]{1,0:T(8,128)S(1)} %get-tuple-element.23), channel_id=1, source_target_pairs={{1,0},{2,1},{3,2},{4,3},{5,4},{6,5},{7,6},{8,7},{9,8},{10,9},{11,1... | collective-permute-start | bytes 835592 | tf_op jit(solution)/shard_map/ppermute | solution.py:475
  19.0 1.3 %collective-permute-start = (f32[17,32,128]{2,1,0:T(8,128)S(1)}, f32[17,32,128]{2,1,0:T(8,128)S(1)}, u32[]{:S(2)}, u32[]{:S(2)}) collective-permute-start(f32[17,32,128]{2,1,0:T(8,128)S(1)} %get-tuple-element.20), channel_id=1, source_target_pairs={{0,32},{32,64},{64,96},{96,128},{128,160},{160,192},{192,224},{224... | collective-permute-start | bytes 835592 | tf_op jit(solution)/shard_map/ppermute | solution.py:474
  20.3 1.3 %collective-permute-start.1 = (f32[17,32,128]{2,1,0:T(8,128)S(1)}, f32[17,32,128]{2,1,0:T(8,128)S(1)}, u32[]{:S(2)}, u32[]{:S(2)}) collective-permute-start(f32[17,32,128]{2,1,0:T(8,128)S(1)} %get-tuple-element.21), channel_id=1, source_target_pairs={{32,0},{64,32},{96,64},{128,96},{160,128},{192,160},{224,192},{256... | collective-permute-start | bytes 835592 | tf_op jit(solution)/shard_map/ppermute | solution.py:475
  21.6 0.0 collective-permute-done.2.low_ref.strip_low
  21.6 0.0 collective-permute-done.3.high_ref.strip_high
  21.6 4.0 %collective-permute-start.4 = (f32[80,128]{1,0:T(8,128)S(1)}, f32[80,128]{1,0:T(8,128)S(1)}, u32[]{:S(2)}, u32[]{:S(2)}) collective-permute-start(f32[80,128]{1,0:T(8,128)S(1)} %get-tuple-element.24), channel_id=1, source_target_pairs={{0,32},{32,64},{64,96},{96,128},{128,160},{160,192},{192,224},{224... | collective-permute-start | bytes 122888 | tf_op jit(solution)/shard_map/ppermute | solution.py:474
  25.6 1.3 %collective-permute-start.5 = (f32[80,128]{1,0:T(8,128)S(1)}, f32[80,128]{1,0:T(8,128)S(1)}, u32[]{:S(2)}, u32[]{:S(2)}) collective-permute-start(f32[80,128]{1,0:T(8,128)S(1)} %get-tuple-element.25), channel_id=1, source_target_pairs={{32,0},{64,32},{96,64},{128,96},{160,128},{192,160},{224,192},{256... | collective-permute-start | bytes 122888 | tf_op jit(solution)/shard_map/ppermute | solution.py:475
  26.9 0.0 collective-permute-done.slab_low
  26.9 3.8 %collective-permute-done.1.slab_high = f32[17,32,128]{2,1,0:T(8,128)S(1)} collective-permute-done((f32[17,32,128]{2,1,0:T(8,128)S(1)}, f32[17,32,128]{2,1,0:T(8,128)S(1)}, u32[]{:S(2)}, u32[]{:S(2)}) %collective-permute-start.1) | collective-permute-done | bytes 278560 | tf_op jit(solution)/shard_map/ppermute | solution.py:475
  30.7 0.0 collective-permute-done.4.corner_low
  30.7 0.7 collective-permute-done.5.corner_high
  31.5 0.0 copy-done.2
  31.5 0.0 copy-done.1
  31.5 0.0 copy-done
  31.5 3.6 %smooth_before.1 = (f32[32,128]{1,0:T(8,128)S(1)}, f32[44,48,128]{2,1,0:T(8,128)S(1)}, f32[44,48,128]{2,1,0:T(8,128)S(1)}, f32[44,48,128]{2,1,0:T(8,128)S(1)}, f...) custom-call(f32[32,32,128]{2,1,0:T(8,128)S(1)} %copy-done, ...), custom_call_target="tpu_custom_call" | custom-call | tf_op jit(solution)/shard_map/smooth_before/pallas_call | solution.py:484
  35.2 10.1 %all_to_all.22 = f32[32,1,128]{2,1,0:T(1,128)S(1)} all-to-all(f32[32,1,128]{2,1,0:T(1,128)S(1)} %bitcast.11), channel_id=1, replica_groups={{11,0,1,2,3,4,5,6,7,8,9,10,12,13,14,15,16,17,18,19,20,21,22,23,24,25,26..., dimensions={0} | all-to-all | bytes 32768 | tf_op jit(solution)/shard_map/all_to_all | solution.py:464
  45.3 33.0 %all_to_all.23 = f32[32,1,128]{2,1,0:T(1,128)S(1)} all-to-all(f32[32,1,128]{2,1,0:T(1,128)S(1)} %bitcast.10), channel_id=1, replica_groups={{512,544,576,608,640,672,704,736,768,800,832,864,896,928,960,992,0,32,6..., dimensions={0} | all-to-all | bytes 32768 | tf_op jit(solution)/shard_map/all_to_all | solution.py:464
  78.2 5.9 %smooth_after.1 = f32[32,32,128]{2,1,0:T(8,128)} custom-call(f32[32,128]{1,0:T(8,128)S(1)} %bitcast.8, f32[44,48,128]{2,1,0:T(8,128)S(1)} %get-tuple-element.27.value_in, f32[44,48,128]{2,1,0:T(8,128)S(1)} %get-tuple-element.28.source_ext, f32[44,48,128]{2,1,0:T(8,128)S(1)} %get-tuple-element.29.face_x, f32[44,48,128]{2,1,0:T(8,128)S(1)} %get-tuple-element.30.face_n, ...), custom_call_target="tpu_custom_call" | custom-call | tf_op jit(solution)/shard_map/smooth_after/pallas_call | solution.py:503
  (2 shorter events, 0.0 us)
Async XLA Ops:
  0.0 31.5 %copy-start.2 = (f32[32,32,128]{2,1,0:T(8,128)S(1)}, f32[32,32,128]{2,1,0:T(8,128)}, u32[]{:S(2)}) copy-start(f32[32,32,128]{2,1,0:T(8,128)} %value_in.1) | copy-start | bytes 1572868
  0.0 31.5 %copy-start.1 = (f32[32,32,128]{2,1,0:T(8,128)S(1)}, f32[32,32,128]{2,1,0:T(8,128)}, u32[]{:S(2)}) copy-start(f32[32,32,128]{2,1,0:T(8,128)} %source_in.1) | copy-start | bytes 1572868
  0.0 31.5 %copy-start = (f32[32,32,128]{2,1,0:T(8,128)S(1)}, f32[32,32,128]{2,1,0:T(8,128)}, u32[]{:S(2)}) copy-start(f32[32,32,128]{2,1,0:T(8,128)} %cond_in.1) | copy-start | bytes 1572868
  1.6 20.0 %collective-permute-start.2 = (f32[544,128]{1,0:T(8,128)S(1)}, f32[544,128]{1,0:T(8,128)S(1)}, u32[]{:S(2)}, u32[]{:S(2)}) collective-permute-start(f32[544,128]{1,0:T(8,128)S(1)} %get-tuple-element.22), channel_id=1, source_target_pairs={{0,1},{1,2},{2,3},{3,4},{4,5},{5,6},{6,7},{7,8},{8,9},{9,10},{10,1... | collective-permute-start | bytes 835592 | tf_op jit(solution)/shard_map/ppermute | solution.py:474
  6.2 15.4 %collective-permute-start.3 = (f32[544,128]{1,0:T(8,128)S(1)}, f32[544,128]{1,0:T(8,128)S(1)}, u32[]{:S(2)}, u32[]{:S(2)}) collective-permute-start(f32[544,128]{1,0:T(8,128)S(1)} %get-tuple-element.23), channel_id=1, source_target_pairs={{1,0},{2,1},{3,2},{4,3},{5,4},{6,5},{7,6},{8,7},{9,8},{10,9},{11,1... | collective-permute-start | bytes 835592 | tf_op jit(solution)/shard_map/ppermute | solution.py:475
  19.0 8.0 %collective-permute-start = (f32[17,32,128]{2,1,0:T(8,128)S(1)}, f32[17,32,128]{2,1,0:T(8,128)S(1)}, u32[]{:S(2)}, u32[]{:S(2)}) collective-permute-start(f32[17,32,128]{2,1,0:T(8,128)S(1)} %get-tuple-element.20), channel_id=1, source_target_pairs={{0,32},{32,64},{64,96},{96,128},{128,160},{160,192},{192,224},{224... | collective-permute-start | bytes 835592 | tf_op jit(solution)/shard_map/ppermute | solution.py:474
  20.3 10.5 %collective-permute-start.1 = (f32[17,32,128]{2,1,0:T(8,128)S(1)}, f32[17,32,128]{2,1,0:T(8,128)S(1)}, u32[]{:S(2)}, u32[]{:S(2)}) collective-permute-start(f32[17,32,128]{2,1,0:T(8,128)S(1)} %get-tuple-element.21), channel_id=1, source_target_pairs={{32,0},{64,32},{96,64},{128,96},{160,128},{192,160},{224,192},{256... | collective-permute-start | bytes 835592 | tf_op jit(solution)/shard_map/ppermute | solution.py:475
  21.6 9.1 %collective-permute-start.4 = (f32[80,128]{1,0:T(8,128)S(1)}, f32[80,128]{1,0:T(8,128)S(1)}, u32[]{:S(2)}, u32[]{:S(2)}) collective-permute-start(f32[80,128]{1,0:T(8,128)S(1)} %get-tuple-element.24), channel_id=1, source_target_pairs={{0,32},{32,64},{64,96},{96,128},{128,160},{160,192},{192,224},{224... | collective-permute-start | bytes 122888 | tf_op jit(solution)/shard_map/ppermute | solution.py:474
  25.6 5.9 %collective-permute-start.5 = (f32[80,128]{1,0:T(8,128)S(1)}, f32[80,128]{1,0:T(8,128)S(1)}, u32[]{:S(2)}, u32[]{:S(2)}) collective-permute-start(f32[80,128]{1,0:T(8,128)S(1)} %get-tuple-element.25), channel_id=1, source_target_pairs={{32,0},{64,32},{96,64},{128,96},{160,128},{192,160},{224,192},{256... | collective-permute-start | bytes 122888 | tf_op jit(solution)/shard_map/ppermute | solution.py:475
